TPU v7x, 1024 devices: a whole 4x4x32 slice. The times are simulated.
1024 devices in a mesh: section: 32 (over y, x, core), expert: 32 (over z).
Axes of the slice: x: 4, y: 4, z: 32, core: 2. Of those that a mesh axis runs over, the one named last changes fastest.
Arguments:
- top_grad: bfloat16 [2, 512, 2048], P(None, 'expert'), may hold values from -6 to 6
- layer_input: bfloat16 [32, 2, 512, 2048], P('section', None, 'expert'), may hold values from -6 to 6
- expert_out: bfloat16 [32, 2, 512, 2, 2048], P('section', None, 'expert'), may hold values from -3 to 3
- router_w: float32 [32, 2048, 8], P('section'), may hold values from -0.375 to 0.375
- expert_ids: int32 [32, 2, 512, 2], P('section', None, 'expert'), may hold values from 0 to 7, as said below
- hidden: bfloat16 [32, 2, 256, 7168], P('section', None, None, 'expert'), may hold values from -0.59765625 to 0.59765625
- down_w: bfloat16 [32, 7168, 2048], P('section', 'expert'), may hold values from -0.0625 to 0.0625
Outputs:
- input_grad: bfloat16 [32, 2, 512, 2048], P('section', None, 'expert')
- router_grad: float32 [32, 2048, 8], P('section')
- hidden_grad: bfloat16 [32, 2, 256, 7168], P('section', None, None, 'expert')
- down_grad: bfloat16 [32, 7168, 2048], P('section', 'expert')
Inputs may be any that keep to these rules, and one draw needn't show every extreme that they name: `expert_ids`: the two experts of a token differ. In each micro-batch, the 16 tokens of one device choose expert 0 at most 8 times, and exactly 8 times in some blocks of every draw.
All inputs are finite; a program needn't handle non-finite values.
Results may differ from a plain program's by a relative error of at most 0.024.
Values may be sent and summed in bfloat16 or wider, within the bound.
No kernel may reach another device: no remote copies, remote signals or barrier semaphores. Data moves between devices by JAX's collectives and lax.ppermute only.
A program may use at most 32 MiB of HBM per device.

v0:
```python
import jax
import jax.numpy as jnp
from jax import lax
from jax.sharding import PartitionSpec as P


def passed_along(value, axis, by):
    count = lax.axis_size(axis)
    pairs = [(i, i + by) for i in range(count) if 0 <= i + by < count]
    return lax.ppermute(value, axis, pairs)


def copy_for_each(value, axis):
    count = lax.axis_size(axis)
    return lax.all_to_all(
        jnp.broadcast_to(value[None], (count, *value.shape)), axis, 0, 0, tiled=True
    )


def taken_together(value, axis):
    return copy_for_each(value, axis).sum(axis=0)


def gate_pair(inputs, weights, chosen):
    logits = jnp.einsum(
        "mtd,de->mte", inputs.astype(jnp.float32), weights, precision=lax.Precision.HIGHEST
    )
    select = (chosen[..., None] == jnp.arange(weights.shape[1], dtype=jnp.int32)).astype(
        jnp.float32
    )
    picked = jnp.sum(select * logits[..., None, :], axis=-1)
    gate_first = jax.nn.sigmoid(picked[..., 0] - picked[..., 1])
    return (gate_first, select)


def backprop(cotangent, inputs, outputs, weights, select, gate_first):
    cot_float = cotangent.astype(jnp.float32)
    gate_dot = jnp.einsum("mtkd,mtd->mtk", outputs, cotangent, preferred_element_type=jnp.float32)
    logit_diff = gate_first * (1.0 - gate_first) * (gate_dot[..., 0] - gate_dot[..., 1])
    logit_grad = logit_diff[..., None] * (select[..., 0, :] - select[..., 1, :])
    passed = cot_float + jnp.einsum(
        "mte,de->mtd", logit_grad, weights, precision=lax.Precision.HIGHEST
    )
    router_part = jnp.einsum(
        "mtd,mte->de", inputs.astype(jnp.float32), logit_grad, precision=lax.Precision.HIGHEST
    )
    return (passed.astype(jnp.bfloat16), router_part)


def dispatch_rows(cotangent, gate_first, chosen, capacity):
    is_zero = (chosen == 0).astype(jnp.float32)
    zero_gate = gate_first * is_zero[..., 0] + (1.0 - gate_first) * is_zero[..., 1]
    routed = is_zero[..., 0] + is_zero[..., 1]
    slot_pos = (jnp.cumsum(routed, axis=-1) - routed).astype(jnp.int32)
    slot_ids = jnp.arange(capacity, dtype=jnp.int32)
    pick_table = (
        (slot_pos[..., None, :] == slot_ids[:, None]) & (routed[..., None, :] > 0.5)
    ).astype(jnp.float32)
    scaled = zero_gate[..., None] * cotangent.astype(jnp.float32)
    rows_out = jnp.einsum("mbcu,mbud->mbcd", pick_table, scaled, precision=lax.Precision.HIGHEST)
    return rows_out.astype(jnp.bfloat16)


def per_device(top_grad, layer_input, expert_out, router_w, expert_ids, hidden, down_w):
    section_count = lax.axis_size("section")
    section_index = lax.axis_index("section")
    micro_count = top_grad.shape[0]
    tok_rows = top_grad.shape[1]
    width = top_grad.shape[2]
    inputs = layer_input[0]
    saved_outs = expert_out[0]
    router = router_w[0]
    chosen = expert_ids[0]
    gate_first, select = gate_pair(inputs, router, chosen)
    is_last = section_index == section_count - 1
    empty_cot = jnp.zeros((micro_count, tok_rows, width), jnp.bfloat16)
    empty_router = jnp.zeros((width, router.shape[1]), jnp.float32)

    def advance_all(moment, totals):
        arrived, section_dy, section_dx, router_acc = totals
        active = moment == section_count - 1 - section_index
        cotangent = jnp.where(is_last, top_grad, arrived)
        passed, router_part = backprop(cotangent, inputs, saved_outs, router, select, gate_first)
        section_dy = jnp.where(active, cotangent, section_dy)
        section_dx = jnp.where(active, passed, section_dx)
        router_acc = router_acc + jnp.where(active, router_part, 0.0)
        arrived = passed_along(passed, "section", -1)
        return (arrived, section_dy, section_dx, router_acc)

    start_state = (empty_cot, empty_cot, empty_cot, empty_router)
    _, section_dy, section_dx, router_acc = lax.fori_loop(
        0, section_count, advance_all, start_state
    )
    total_tokens = micro_count * tok_rows * lax.axis_size("expert")
    router_grad = taken_together(router_acc, "expert") / total_tokens
    capacity = tok_rows // 2
    rows_out = dispatch_rows(section_dy[:, None], gate_first[:, None], chosen[:, None], capacity)
    rows_out = rows_out.reshape(micro_count, capacity, width)
    saved_hidden = hidden[0]
    weight = down_w[0]
    ff_local = weight.shape[0]
    slot_total = saved_hidden.shape[1]
    gathered = lax.all_gather(rows_out, "expert", axis=1, tiled=True)
    flat_rows = gathered.reshape(-1, width)
    hidden_acc = lax.dot_general(
        flat_rows, weight, (((1,), (1,)), ((), ())), preferred_element_type=jnp.float32
    )
    hidden_acc = hidden_acc.astype(jnp.bfloat16).reshape(micro_count, slot_total, ff_local)
    weight_sum = lax.dot_general(
        saved_hidden.reshape(-1, ff_local),
        flat_rows,
        (((0,), (0,)), ((), ())),
        preferred_element_type=jnp.float32,
    )
    return (
        section_dx[None],
        router_grad[None],
        hidden_acc[None],
        weight_sum.astype(jnp.bfloat16)[None],
    )


def solution(mesh):
    placed = (
        P(None, "expert", None),
        P("section", None, "expert", None),
        P("section", None, "expert", None, None),
        P("section", None, None),
        P("section", None, "expert", None),
        P("section", None, None, "expert"),
        P("section", "expert", None),
    )
    return jax.shard_map(
        per_device,
        mesh=mesh,
        in_specs=placed,
        out_specs=(
            P("section", None, "expert", None),
            P("section", None, None),
            P("section", None, None, "expert"),
            P("section", "expert", None),
        ),
        check_vma=False,
    )
```

profile of v0, /device:TPU:46, one launch (start us, length us, event | category | flops | bytes accessed | tf_op | source)
XLA Modules:
  0.0 626.7 jit_solution(7546237376384166069)
XLA Ops:
  9.5 335.1 %while.22 = (s32[]{:T(128)}, bf16[2,16,2048]{2,1,0:T(8,128)(2,1)S(1)}, bf16[2,16,2048]{2,1,0:T(8,128)(2,1)S(1)}, bf16[2,16,2048]{2,1,0:T(8,128)(2,1)S(1)}, f32[2...) while((s32[]{:T(128)}, ...), condition=%wide.region_2.3_spmd.clone, body=%wide.region_1.2_spmd.clone.sunk | while | flops 13419140 | bytes 3215110 | solution.py:91
  40.1 6.2 collective-permute-done
  50.8 6.2 collective-permute-done
  61.4 6.2 collective-permute-done
  72.1 6.2 collective-permute-done
  82.7 6.2 collective-permute-done
  93.4 6.2 collective-permute-done
  104.1 6.2 collective-permute-done
  114.7 6.2 collective-permute-done
  125.4 6.2 collective-permute-done
  136.0 6.2 collective-permute-done
  146.7 6.2 collective-permute-done
  157.3 6.2 collective-permute-done
  168.0 6.2 collective-permute-done
  178.6 6.2 collective-permute-done
  189.3 6.2 collective-permute-done
  199.9 6.2 collective-permute-done
  210.6 6.2 collective-permute-done
  221.2 6.2 collective-permute-done
  231.9 6.2 collective-permute-done
  242.5 6.2 collective-permute-done
  253.2 6.2 collective-permute-done
  263.8 6.2 collective-permute-done
  274.5 6.2 collective-permute-done
  285.1 6.2 collective-permute-done
  295.8 6.2 collective-permute-done
  306.5 6.2 collective-permute-done
  317.1 6.2 collective-permute-done
  327.8 6.2 collective-permute-done
  338.4 6.2 collective-permute-done
  346.2 28.7 %all-to-all-start = ((f32[32,2048,8]{1,2,0:T(8,128)}), f32[32,2048,8]{1,2,0:T(8,128)S(1)}, u32[]{:S(2)}, u32[]{:S(2)}) async-start(f32[32,2048,8]{1,2,0:T(8,128)} %broadcast_in_dim.42), calls=%async_computation | async-start | bytes 4194304 | tf_op jit(solution)/shard_map/all_to_all | solution.py:15
  376.5 234.6 %all-gather.2.cloned.1.call-done = bf16[2,256,2048]{2,1,0:T(8,128)(2,1)} async-done(((bf16[2,8,2048]{2,1,0:T(8,128)(2,1)}), bf16[2,256,2048]{2,1,0:T(8,128)(2,1)}) %all-gather.2.cloned.1.call-update) | async-done | bytes 2097168 | tf_op jit(solution)/shard_map/all_gather | solution.py:103
  (392 shorter events, 167.7 us)
Async XLA Ops:
  27.3 8.4 %collective-permute-start = (bf16[2,16,2048]{2,1,0:T(8,128)(2,1)S(1)}, bf16[2,16,2048]{2,1,0:T(8,128)(2,1)S(1)}, u32[]{:S(2)}, u32[]{:S(2)}) collective-permute-start(bf16[2,16,2048]{2,1,0:T(8,128)(2,1)S(1)} %get-tuple-element.477), channel_id=1, source_target_pairs={{32,0},{64,32},{96,64},{128,96},{160,128},{192,160},{224,192},{256... | collective-permute-start | bytes 393224 | tf_op jit(solution)/shard_map/while/body/eval_jaxpr/ppermute | solution.py:10
  37.9 8.4 %collective-permute-start = (bf16[2,16,2048]{2,1,0:T(8,128)(2,1)S(1)}, bf16[2,16,2048]{2,1,0:T(8,128)(2,1)S(1)}, u32[]{:S(2)}, u32[]{:S(2)}) collective-permute-start(bf16[2,16,2048]{2,1,0:T(8,128)(2,1)S(1)} %get-tuple-element.477), channel_id=1, source_target_pairs={{32,0},{64,32},{96,64},{128,96},{160,128},{192,160},{224,192},{256... | collective-permute-start | bytes 393224 | tf_op jit(solution)/shard_map/while/body/eval_jaxpr/ppermute | solution.py:10
  48.6 8.4 %collective-permute-start = (bf16[2,16,2048]{2,1,0:T(8,128)(2,1)S(1)}, bf16[2,16,2048]{2,1,0:T(8,128)(2,1)S(1)}, u32[]{:S(2)}, u32[]{:S(2)}) collective-permute-start(bf16[2,16,2048]{2,1,0:T(8,128)(2,1)S(1)} %get-tuple-element.477), channel_id=1, source_target_pairs={{32,0},{64,32},{96,64},{128,96},{160,128},{192,160},{224,192},{256... | collective-permute-start | bytes 393224 | tf_op jit(solution)/shard_map/while/body/eval_jaxpr/ppermute | solution.py:10
  59.3 8.4 %collective-permute-start = (bf16[2,16,2048]{2,1,0:T(8,128)(2,1)S(1)}, bf16[2,16,2048]{2,1,0:T(8,128)(2,1)S(1)}, u32[]{:S(2)}, u32[]{:S(2)}) collective-permute-start(bf16[2,16,2048]{2,1,0:T(8,128)(2,1)S(1)} %get-tuple-element.477), channel_id=1, source_target_pairs={{32,0},{64,32},{96,64},{128,96},{160,128},{192,160},{224,192},{256... | collective-permute-start | bytes 393224 | tf_op jit(solution)/shard_map/while/body/eval_jaxpr/ppermute | solution.py:10
  69.9 8.4 %collective-permute-start = (bf16[2,16,2048]{2,1,0:T(8,128)(2,1)S(1)}, bf16[2,16,2048]{2,1,0:T(8,128)(2,1)S(1)}, u32[]{:S(2)}, u32[]{:S(2)}) collective-permute-start(bf16[2,16,2048]{2,1,0:T(8,128)(2,1)S(1)} %get-tuple-element.477), channel_id=1, source_target_pairs={{32,0},{64,32},{96,64},{128,96},{160,128},{192,160},{224,192},{256... | collective-permute-start | bytes 393224 | tf_op jit(solution)/shard_map/while/body/eval_jaxpr/ppermute | solution.py:10
  80.6 8.4 %collective-permute-start = (bf16[2,16,2048]{2,1,0:T(8,128)(2,1)S(1)}, bf16[2,16,2048]{2,1,0:T(8,128)(2,1)S(1)}, u32[]{:S(2)}, u32[]{:S(2)}) collective-permute-start(bf16[2,16,2048]{2,1,0:T(8,128)(2,1)S(1)} %get-tuple-element.477), channel_id=1, source_target_pairs={{32,0},{64,32},{96,64},{128,96},{160,128},{192,160},{224,192},{256... | collective-permute-start | bytes 393224 | tf_op jit(solution)/shard_map/while/body/eval_jaxpr/ppermute | solution.py:10
  91.2 8.4 %collective-permute-start = (bf16[2,16,2048]{2,1,0:T(8,128)(2,1)S(1)}, bf16[2,16,2048]{2,1,0:T(8,128)(2,1)S(1)}, u32[]{:S(2)}, u32[]{:S(2)}) collective-permute-start(bf16[2,16,2048]{2,1,0:T(8,128)(2,1)S(1)} %get-tuple-element.477), channel_id=1, source_target_pairs={{32,0},{64,32},{96,64},{128,96},{160,128},{192,160},{224,192},{256... | collective-permute-start | bytes 393224 | tf_op jit(solution)/shard_map/while/body/eval_jaxpr/ppermute | solution.py:10
  101.9 8.4 %collective-permute-start = (bf16[2,16,2048]{2,1,0:T(8,128)(2,1)S(1)}, bf16[2,16,2048]{2,1,0:T(8,128)(2,1)S(1)}, u32[]{:S(2)}, u32[]{:S(2)}) collective-permute-start(bf16[2,16,2048]{2,1,0:T(8,128)(2,1)S(1)} %get-tuple-element.477), channel_id=1, source_target_pairs={{32,0},{64,32},{96,64},{128,96},{160,128},{192,160},{224,192},{256... | collective-permute-start | bytes 393224 | tf_op jit(solution)/shard_map/while/body/eval_jaxpr/ppermute | solution.py:10
  112.5 8.4 %collective-permute-start = (bf16[2,16,2048]{2,1,0:T(8,128)(2,1)S(1)}, bf16[2,16,2048]{2,1,0:T(8,128)(2,1)S(1)}, u32[]{:S(2)}, u32[]{:S(2)}) collective-permute-start(bf16[2,16,2048]{2,1,0:T(8,128)(2,1)S(1)} %get-tuple-element.477), channel_id=1, source_target_pairs={{32,0},{64,32},{96,64},{128,96},{160,128},{192,160},{224,192},{256... | collective-permute-start | bytes 393224 | tf_op jit(solution)/shard_map/while/body/eval_jaxpr/ppermute | solution.py:10
  123.2 8.4 %collective-permute-start = (bf16[2,16,2048]{2,1,0:T(8,128)(2,1)S(1)}, bf16[2,16,2048]{2,1,0:T(8,128)(2,1)S(1)}, u32[]{:S(2)}, u32[]{:S(2)}) collective-permute-start(bf16[2,16,2048]{2,1,0:T(8,128)(2,1)S(1)} %get-tuple-element.477), channel_id=1, source_target_pairs={{32,0},{64,32},{96,64},{128,96},{160,128},{192,160},{224,192},{256... | collective-permute-start | bytes 393224 | tf_op jit(solution)/shard_map/while/body/eval_jaxpr/ppermute | solution.py:10
  133.8 8.4 %collective-permute-start = (bf16[2,16,2048]{2,1,0:T(8,128)(2,1)S(1)}, bf16[2,16,2048]{2,1,0:T(8,128)(2,1)S(1)}, u32[]{:S(2)}, u32[]{:S(2)}) collective-permute-start(bf16[2,16,2048]{2,1,0:T(8,128)(2,1)S(1)} %get-tuple-element.477), channel_id=1, source_target_pairs={{32,0},{64,32},{96,64},{128,96},{160,128},{192,160},{224,192},{256... | collective-permute-start | bytes 393224 | tf_op jit(solution)/shard_map/while/body/eval_jaxpr/ppermute | solution.py:10
  144.5 8.4 %collective-permute-start = (bf16[2,16,2048]{2,1,0:T(8,128)(2,1)S(1)}, bf16[2,16,2048]{2,1,0:T(8,128)(2,1)S(1)}, u32[]{:S(2)}, u32[]{:S(2)}) collective-permute-start(bf16[2,16,2048]{2,1,0:T(8,128)(2,1)S(1)} %get-tuple-element.477), channel_id=1, source_target_pairs={{32,0},{64,32},{96,64},{128,96},{160,128},{192,160},{224,192},{256... | collective-permute-start | bytes 393224 | tf_op jit(solution)/shard_map/while/body/eval_jaxpr/ppermute | solution.py:10
  155.1 8.4 %collective-permute-start = (bf16[2,16,2048]{2,1,0:T(8,128)(2,1)S(1)}, bf16[2,16,2048]{2,1,0:T(8,128)(2,1)S(1)}, u32[]{:S(2)}, u32[]{:S(2)}) collective-permute-start(bf16[2,16,2048]{2,1,0:T(8,128)(2,1)S(1)} %get-tuple-element.477), channel_id=1, source_target_pairs={{32,0},{64,32},{96,64},{128,96},{160,128},{192,160},{224,192},{256... | collective-permute-start | bytes 393224 | tf_op jit(solution)/shard_map/while/body/eval_jaxpr/ppermute | solution.py:10
  165.8 8.4 %collective-permute-start = (bf16[2,16,2048]{2,1,0:T(8,128)(2,1)S(1)}, bf16[2,16,2048]{2,1,0:T(8,128)(2,1)S(1)}, u32[]{:S(2)}, u32[]{:S(2)}) collective-permute-start(bf16[2,16,2048]{2,1,0:T(8,128)(2,1)S(1)} %get-tuple-element.477), channel_id=1, source_target_pairs={{32,0},{64,32},{96,64},{128,96},{160,128},{192,160},{224,192},{256... | collective-permute-start | bytes 393224 | tf_op jit(solution)/shard_map/while/body/eval_jaxpr/ppermute | solution.py:10
  176.4 8.4 %collective-permute-start = (bf16[2,16,2048]{2,1,0:T(8,128)(2,1)S(1)}, bf16[2,16,2048]{2,1,0:T(8,128)(2,1)S(1)}, u32[]{:S(2)}, u32[]{:S(2)}) collective-permute-start(bf16[2,16,2048]{2,1,0:T(8,128)(2,1)S(1)} %get-tuple-element.477), channel_id=1, source_target_pairs={{32,0},{64,32},{96,64},{128,96},{160,128},{192,160},{224,192},{256... | collective-permute-start | bytes 393224 | tf_op jit(solution)/shard_map/while/body/eval_jaxpr/ppermute | solution.py:10
  187.1 8.4 %collective-permute-start = (bf16[2,16,2048]{2,1,0:T(8,128)(2,1)S(1)}, bf16[2,16,2048]{2,1,0:T(8,128)(2,1)S(1)}, u32[]{:S(2)}, u32[]{:S(2)}) collective-permute-start(bf16[2,16,2048]{2,1,0:T(8,128)(2,1)S(1)} %get-tuple-element.477), channel_id=1, source_target_pairs={{32,0},{64,32},{96,64},{128,96},{160,128},{192,160},{224,192},{256... | collective-permute-start | bytes 393224 | tf_op jit(solution)/shard_map/while/body/eval_jaxpr/ppermute | solution.py:10
  197.7 8.4 %collective-permute-start = (bf16[2,16,2048]{2,1,0:T(8,128)(2,1)S(1)}, bf16[2,16,2048]{2,1,0:T(8,128)(2,1)S(1)}, u32[]{:S(2)}, u32[]{:S(2)}) collective-permute-start(bf16[2,16,2048]{2,1,0:T(8,128)(2,1)S(1)} %get-tuple-element.477), channel_id=1, source_target_pairs={{32,0},{64,32},{96,64},{128,96},{160,128},{192,160},{224,192},{256... | collective-permute-start | bytes 393224 | tf_op jit(solution)/shard_map/while/body/eval_jaxpr/ppermute | solution.py:10
  208.4 8.4 %collective-permute-start = (bf16[2,16,2048]{2,1,0:T(8,128)(2,1)S(1)}, bf16[2,16,2048]{2,1,0:T(8,128)(2,1)S(1)}, u32[]{:S(2)}, u32[]{:S(2)}) collective-permute-start(bf16[2,16,2048]{2,1,0:T(8,128)(2,1)S(1)} %get-tuple-element.477), channel_id=1, source_target_pairs={{32,0},{64,32},{96,64},{128,96},{160,128},{192,160},{224,192},{256... | collective-permute-start | bytes 393224 | tf_op jit(solution)/shard_map/while/body/eval_jaxpr/ppermute | solution.py:10
  219.0 8.4 %collective-permute-start = (bf16[2,16,2048]{2,1,0:T(8,128)(2,1)S(1)}, bf16[2,16,2048]{2,1,0:T(8,128)(2,1)S(1)}, u32[]{:S(2)}, u32[]{:S(2)}) collective-permute-start(bf16[2,16,2048]{2,1,0:T(8,128)(2,1)S(1)} %get-tuple-element.477), channel_id=1, source_target_pairs={{32,0},{64,32},{96,64},{128,96},{160,128},{192,160},{224,192},{256... | collective-permute-start | bytes 393224 | tf_op jit(solution)/shard_map/while/body/eval_jaxpr/ppermute | solution.py:10
  229.7 8.4 %collective-permute-start = (bf16[2,16,2048]{2,1,0:T(8,128)(2,1)S(1)}, bf16[2,16,2048]{2,1,0:T(8,128)(2,1)S(1)}, u32[]{:S(2)}, u32[]{:S(2)}) collective-permute-start(bf16[2,16,2048]{2,1,0:T(8,128)(2,1)S(1)} %get-tuple-element.477), channel_id=1, source_target_pairs={{32,0},{64,32},{96,64},{128,96},{160,128},{192,160},{224,192},{256... | collective-permute-start | bytes 393224 | tf_op jit(solution)/shard_map/while/body/eval_jaxpr/ppermute | solution.py:10
  240.4 8.4 %collective-permute-start = (bf16[2,16,2048]{2,1,0:T(8,128)(2,1)S(1)}, bf16[2,16,2048]{2,1,0:T(8,128)(2,1)S(1)}, u32[]{:S(2)}, u32[]{:S(2)}) collective-permute-start(bf16[2,16,2048]{2,1,0:T(8,128)(2,1)S(1)} %get-tuple-element.477), channel_id=1, source_target_pairs={{32,0},{64,32},{96,64},{128,96},{160,128},{192,160},{224,192},{256... | collective-permute-start | bytes 393224 | tf_op jit(solution)/shard_map/while/body/eval_jaxpr/ppermute | solution.py:10
  251.0 8.4 %collective-permute-start = (bf16[2,16,2048]{2,1,0:T(8,128)(2,1)S(1)}, bf16[2,16,2048]{2,1,0:T(8,128)(2,1)S(1)}, u32[]{:S(2)}, u32[]{:S(2)}) collective-permute-start(bf16[2,16,2048]{2,1,0:T(8,128)(2,1)S(1)} %get-tuple-element.477), channel_id=1, source_target_pairs={{32,0},{64,32},{96,64},{128,96},{160,128},{192,160},{224,192},{256... | collective-permute-start | bytes 393224 | tf_op jit(solution)/shard_map/while/body/eval_jaxpr/ppermute | solution.py:10
  261.7 8.4 %collective-permute-start = (bf16[2,16,2048]{2,1,0:T(8,128)(2,1)S(1)}, bf16[2,16,2048]{2,1,0:T(8,128)(2,1)S(1)}, u32[]{:S(2)}, u32[]{:S(2)}) collective-permute-start(bf16[2,16,2048]{2,1,0:T(8,128)(2,1)S(1)} %get-tuple-element.477), channel_id=1, source_target_pairs={{32,0},{64,32},{96,64},{128,96},{160,128},{192,160},{224,192},{256... | collective-permute-start | bytes 393224 | tf_op jit(solution)/shard_map/while/body/eval_jaxpr/ppermute | solution.py:10
  272.3 8.4 %collective-permute-start = (bf16[2,16,2048]{2,1,0:T(8,128)(2,1)S(1)}, bf16[2,16,2048]{2,1,0:T(8,128)(2,1)S(1)}, u32[]{:S(2)}, u32[]{:S(2)}) collective-permute-start(bf16[2,16,2048]{2,1,0:T(8,128)(2,1)S(1)} %get-tuple-element.477), channel_id=1, source_target_pairs={{32,0},{64,32},{96,64},{128,96},{160,128},{192,160},{224,192},{256... | collective-permute-start | bytes 393224 | tf_op jit(solution)/shard_map/while/body/eval_jaxpr/ppermute | solution.py:10
  283.0 8.4 %collective-permute-start = (bf16[2,16,2048]{2,1,0:T(8,128)(2,1)S(1)}, bf16[2,16,2048]{2,1,0:T(8,128)(2,1)S(1)}, u32[]{:S(2)}, u32[]{:S(2)}) collective-permute-start(bf16[2,16,2048]{2,1,0:T(8,128)(2,1)S(1)} %get-tuple-element.477), channel_id=1, source_target_pairs={{32,0},{64,32},{96,64},{128,96},{160,128},{192,160},{224,192},{256... | collective-permute-start | bytes 393224 | tf_op jit(solution)/shard_map/while/body/eval_jaxpr/ppermute | solution.py:10
  293.6 8.4 %collective-permute-start = (bf16[2,16,2048]{2,1,0:T(8,128)(2,1)S(1)}, bf16[2,16,2048]{2,1,0:T(8,128)(2,1)S(1)}, u32[]{:S(2)}, u32[]{:S(2)}) collective-permute-start(bf16[2,16,2048]{2,1,0:T(8,128)(2,1)S(1)} %get-tuple-element.477), channel_id=1, source_target_pairs={{32,0},{64,32},{96,64},{128,96},{160,128},{192,160},{224,192},{256... | collective-permute-start | bytes 393224 | tf_op jit(solution)/shard_map/while/body/eval_jaxpr/ppermute | solution.py:10
  304.3 8.4 %collective-permute-start = (bf16[2,16,2048]{2,1,0:T(8,128)(2,1)S(1)}, bf16[2,16,2048]{2,1,0:T(8,128)(2,1)S(1)}, u32[]{:S(2)}, u32[]{:S(2)}) collective-permute-start(bf16[2,16,2048]{2,1,0:T(8,128)(2,1)S(1)} %get-tuple-element.477), channel_id=1, source_target_pairs={{32,0},{64,32},{96,64},{128,96},{160,128},{192,160},{224,192},{256... | collective-permute-start | bytes 393224 | tf_op jit(solution)/shard_map/while/body/eval_jaxpr/ppermute | solution.py:10
  314.9 8.4 %collective-permute-start = (bf16[2,16,2048]{2,1,0:T(8,128)(2,1)S(1)}, bf16[2,16,2048]{2,1,0:T(8,128)(2,1)S(1)}, u32[]{:S(2)}, u32[]{:S(2)}) collective-permute-start(bf16[2,16,2048]{2,1,0:T(8,128)(2,1)S(1)} %get-tuple-element.477), channel_id=1, source_target_pairs={{32,0},{64,32},{96,64},{128,96},{160,128},{192,160},{224,192},{256... | collective-permute-start | bytes 393224 | tf_op jit(solution)/shard_map/while/body/eval_jaxpr/ppermute | solution.py:10
  325.6 8.4 %collective-permute-start = (bf16[2,16,2048]{2,1,0:T(8,128)(2,1)S(1)}, bf16[2,16,2048]{2,1,0:T(8,128)(2,1)S(1)}, u32[]{:S(2)}, u32[]{:S(2)}) collective-permute-start(bf16[2,16,2048]{2,1,0:T(8,128)(2,1)S(1)} %get-tuple-element.477), channel_id=1, source_target_pairs={{32,0},{64,32},{96,64},{128,96},{160,128},{192,160},{224,192},{256... | collective-permute-start | bytes 393224 | tf_op jit(solution)/shard_map/while/body/eval_jaxpr/ppermute | solution.py:10
  336.2 8.4 %collective-permute-start = (bf16[2,16,2048]{2,1,0:T(8,128)(2,1)S(1)}, bf16[2,16,2048]{2,1,0:T(8,128)(2,1)S(1)}, u32[]{:S(2)}, u32[]{:S(2)}) collective-permute-start(bf16[2,16,2048]{2,1,0:T(8,128)(2,1)S(1)} %get-tuple-element.477), channel_id=1, source_target_pairs={{32,0},{64,32},{96,64},{128,96},{160,128},{192,160},{224,192},{256... | collective-permute-start | bytes 393224 | tf_op jit(solution)/shard_map/while/body/eval_jaxpr/ppermute | solution.py:10
  346.2 272.9 %all-to-all-start = ((f32[32,2048,8]{1,2,0:T(8,128)}), f32[32,2048,8]{1,2,0:T(8,128)S(1)}, u32[]{:S(2)}, u32[]{:S(2)}) async-start(f32[32,2048,8]{1,2,0:T(8,128)} %broadcast_in_dim.42), calls=%async_computation | async-start | bytes 4194304 | tf_op jit(solution)/shard_map/all_to_all | solution.py:15
  375.0 236.1 %all-gather.2.cloned.1.call-start = ((), (), s32[]{:S(2)}) async-start(), calls=%async_computation.1 | async-start | bytes 2162688 | tf_op jit(solution)/shard_map/all_gather | solution.py:103
  (70 other events, 871.0 us)
Sparse Core Ops, SparseCore 0:
  379.0 232.0 all-gather.1
where the time goes:
time: 629 us; the launch traced here: 627 us
  waiting for transfers between devices  423 us (67%)
  starting transfers between devices  94.2 us (15%)
  matrix products  82.5 us (13%)
  between operations  14.2 us (2%)
  local copies, waits for them, and re-layouts  7.41 us (1%)
    all_gather x1, waiting for transfers between devices, per_device(): gathered = lax.all_gather(rows_out, 'expert', axis=1, tiled=True)  235 us
    ppermute x32, waiting for transfers between devices, passed_along(): return lax.ppermute(value, axis, pairs)  189 us
    ppermute x32, starting transfers between devices, passed_along(): return lax.ppermute(value, axis, pairs)  65.4 us
    dot_general x32, matrix products, backprop(): jnp.einsum('mtkd,mtd->mtk', outputs, cotangent, preferred_element_type=jn...  51.9 us
    all_to_all x1, starting transfers between devices, copy_for_each(): lax.all_to_all(jnp.broadcast_to(value[None], (count, *value.shape)), axis...  28.7 us
    dot_general x32, matrix products, backprop(): jnp.einsum('mte,de->mtd', logit_grad, weights, precision=lax.Precision.HI...  14.2 us
  transfers between devices with their start and end apart: 34, of which 33 were waited for; matrix products, arithmetic and copies ran while one was open for 3% of the time, Pallas kernels for 0%

commit v1 on v0

v1 whole, which is shorter than its diff:
```python
import jax
import jax.numpy as jnp
from jax import lax
from jax.experimental import pallas as pl
from jax.experimental.pallas import tpu as pltpu
from jax.sharding import PartitionSpec as P

HIGH = lax.Precision.HIGHEST


def cascade_kernel(ur_ref, top_ref, out_ref):
    count = ur_ref.shape[0]
    cot = top_ref[0].astype(jnp.float32)
    for layer in reversed(range(count)):
        out_ref[layer] = cot.astype(jnp.bfloat16)
        if layer:
            prod = ur_ref[layer, 0].astype(jnp.float32) * cot
            half = prod[:, :128] + prod[:, 128:]
            diff = jnp.sum(jnp.sum(half, axis=1, keepdims=True), axis=0, keepdims=True)
            cot = cot + diff * ur_ref[layer, 1].astype(jnp.float32)
            cot = cot.astype(jnp.bfloat16).astype(jnp.float32)


def cascade(pairs, top_token):
    count = pairs.shape[0]
    return pl.pallas_call(
        cascade_kernel,
        out_shape=jax.ShapeDtypeStruct((count, 8, 256), jnp.bfloat16),
        name="cascade",
    )(pairs, top_token)


def swap(value):
    return lax.all_to_all(value, "section", 0, 0, tiled=True)


def to_half(value):
    peak = jnp.max(jnp.abs(value), axis=-1, keepdims=True)
    power = jnp.clip(jnp.ceil(jnp.log2(jnp.maximum(peak, 1e-30))), -100.0, 120.0)
    return (value * jnp.exp2(-power)).astype(jnp.float16), power[..., 0]


def per_device(top_grad, layer_input, expert_out, router_w, expert_ids, hidden, down_w):
    micro, tok, width = top_grad.shape
    tokens = micro * tok
    sections = lax.axis_size("section")
    groups = lax.axis_size("expert")
    capacity = tok // 2
    inputs = layer_input[0].reshape(tokens, width).astype(jnp.float32)
    outputs = expert_out[0].reshape(tokens, 2, width)
    router = router_w[0]
    experts = router.shape[1]
    chosen = expert_ids[0].reshape(tokens, 2)

    logits = jnp.dot(inputs, router, precision=HIGH)
    select = (chosen[..., None] == jnp.arange(experts, dtype=jnp.int32)).astype(jnp.float32)
    sign = select[:, 0] - select[:, 1]
    gate = jax.nn.sigmoid(jnp.sum(sign * logits, axis=-1))
    slope = gate * (1.0 - gate)
    out_diff = outputs[:, 0].astype(jnp.float32) - outputs[:, 1].astype(jnp.float32)
    step = lax.dot_general(sign, router, (((1,), (1,)), ((), ())), precision=HIGH)

    pairs = jnp.stack(
        [(slope[:, None] * out_diff).astype(jnp.bfloat16), step.astype(jnp.bfloat16)], axis=1
    ).reshape(tokens, 2, 8, width // 8)
    mine = lax.axis_index("section")
    top_token = lax.dynamic_slice_in_dim(top_grad.reshape(tokens, width), mine, 1, 0)
    cots = cascade(swap(pairs), top_token.reshape(1, 8, width // 8))
    cot = swap(cots).reshape(tokens, width).astype(jnp.float32)

    logit_diff = slope * jnp.sum(out_diff * cot, axis=-1)
    input_grad = (cot + logit_diff[:, None] * step).astype(jnp.bfloat16)
    logit_grad = logit_diff[:, None] * sign
    router_part = lax.dot_general(
        logit_grad[:, 1:], inputs, (((0,), (0,)), ((), ())), precision=HIGH
    )

    is_zero = (chosen == 0).astype(jnp.float32)
    zero_gate = gate * is_zero[:, 0] + (1.0 - gate) * is_zero[:, 1]
    routed = (is_zero[:, 0] + is_zero[:, 1]).reshape(micro, tok)
    earlier = jnp.tril(jnp.ones((tok, tok), jnp.float32), -1)
    slot_pos = jnp.sum(routed[:, None, :] * earlier, axis=-1).astype(jnp.int32)
    slot_ids = jnp.arange(capacity, dtype=jnp.int32)
    pick = ((slot_pos[:, None, :] == slot_ids[:, None]) & (routed[:, None, :] > 0.5)).astype(
        jnp.float32
    )
    scaled = (zero_gate[:, None] * cot).reshape(micro, tok, width)
    rows = jnp.einsum("mcu,mud->mcd", pick, scaled, precision=HIGH).astype(jnp.bfloat16)

    held = jnp.concatenate(
        [rows.reshape(micro * capacity, width).astype(jnp.float32), router_part], axis=0
    )
    half, power = to_half(held)
    powers = jnp.zeros((1, width), jnp.float16)
    powers = lax.dynamic_update_slice(powers, power[None].astype(jnp.float16), (0, 0))
    sent = jnp.concatenate([half, powers], axis=0)
    got = lax.all_gather(sent, "expert", axis=0, tiled=False)

    scale = jnp.exp2(got[:, -1, : micro * capacity + experts - 1].astype(jnp.float32))

    def received(first, size):
        part = got[:, first : first + size].astype(jnp.float32)
        return part * scale[:, first : first + size, None]

    others = jnp.sum(received(micro * capacity, experts - 1), axis=0)
    router_sum = jnp.concatenate([-jnp.sum(others, axis=0, keepdims=True), others], axis=0)
    router_grad = router_sum.T / (tokens * groups)

    weight = down_w[0]
    hidden_parts = []
    down_acc = 0.0
    for part in range(micro):
        slots = received(part * capacity, capacity).astype(jnp.bfloat16).reshape(-1, width)
        hidden_parts.append(
            lax.dot_general(
                weight, slots, (((1,), (1,)), ((), ())), preferred_element_type=jnp.float32
            ).astype(jnp.bfloat16)
        )
        down_acc = down_acc + lax.dot_general(
            hidden[0, part], slots, (((0,), (0,)), ((), ())), preferred_element_type=jnp.float32
        )
    hidden_grad = jnp.stack(hidden_parts).transpose(0, 2, 1)
    down_grad = down_acc
    return (
        input_grad.reshape(1, micro, tok, width),
        router_grad[None],
        hidden_grad[None],
        down_grad.astype(jnp.bfloat16)[None],
    )


def solution(mesh):
    placed = (
        P(None, "expert", None),
        P("section", None, "expert", None),
        P("section", None, "expert", None, None),
        P("section", None, None),
        P("section", None, "expert", None),
        P("section", None, None, "expert"),
        P("section", "expert", None),
    )
    return jax.shard_map(
        per_device,
        mesh=mesh,
        in_specs=placed,
        out_specs=(
            P("section", None, "expert", None),
            P("section", None, None),
            P("section", None, None, "expert"),
            P("section", "expert", None),
        ),
        check_vma=False,
    )
```

time: 629 us -> 134 us (0.21)
  the two profiles are of different devices: /device:TPU:46 before, /device:TPU:2 now
where the time goes in v1:
time: 134 us
  blocking collectives  79.6 us (59%)
  starting transfers between devices  21.8 us (16%)
  waiting for transfers between devices  12.5 us (9%)
  matrix products  6.14 us (5%)
  local copies, waits for them, and re-layouts  4.77 us (4%)
  Pallas kernels  4.32 us (3%)
  other arithmetic  4 us (3%)
    all_gather x1, blocking collectives, per_device(): got = lax.all_gather(sent, 'expert', axis=0, tiled=False)  79.6 us
    all_to_all x2, starting transfers between devices, swap(): return lax.all_to_all(value, 'section', 0, 0, tiled=True)  21.8 us
    all_to_all x2, waiting for transfers between devices, swap(): return lax.all_to_all(value, 'section', 0, 0, tiled=True)  12.5 us
    pallas_call x1, Pallas kernels, cascade(): pl.pallas_call(cascade_kernel, out_shape=jax.ShapeDtypeStruct((count, 8,...  4.32 us
    unnamed x13, local copies, waits for them, and re-layouts  2.93 us
  transfers between devices with their start and end apart: 2, of which 2 were waited for; matrix products, arithmetic and copies ran while one was open for 1% of the time, Pallas kernels for 0%

profile of v1, /device:TPU:2, one launch (start us, length us, event | category | flops | bytes accessed | tf_op | source)
XLA Modules:
  0.0 134.0 jit_solution(6468681967594495747)
XLA Ops:
  0.6 0.8 copy.13
  1.4 0.1 eq.34
  1.5 1.2 fusion.48
  2.8 1.1 fusion.8
  3.9 1.0 copy.14
  5.0 0.1 multiply_convert_fusion.2
  5.1 0.7 pad_maximum_fusion
  5.9 16.7 %all-to-all-start = ((bf16[32,2,8,256]{3,2,1,0:T(8,128)(2,1)}), bf16[32,2,8,256]{3,2,1,0:T(8,128)(2,1)S(1)}, u32[]{:S(2)}, u32[]{:S(2)}) async-start(bf16[32,2,8,256]{3,2,1,0:T(8,128)(2,1)} %pad_maximum_fusion), calls=%async_computation | async-start | bytes 524288 | tf_op jit(solution)/shard_map/all_to_all | solution.py:34
  22.6 0.8 dynamic-slice_reduce_fusion
  23.4 0.6 reshape.194.top_ref
  24.2 0.1 multiply_reduce_fusion
  24.3 5.9 %all-to-all-done.ur_ref = bf16[32,2,8,256]{3,2,1,0:T(8,128)(2,1)S(1)} async-done(((bf16[32,2,8,256]{3,2,1,0:T(8,128)(2,1)}), bf16[32,2,8,256]{3,2,1,0:T(8,128)(2,1)S(1)}, u32[]{:S(2)}, u32[]{:S(2)}) %all-to-all-start) | async-done | bytes 262176 | tf_op jit(solution)/shard_map/all_to_all | solution.py:34
  30.3 0.7 copy-done.1
  31.0 4.3 %cascade.1 = bf16[32,8,256]{2,1,0:T(8,128)(2,1)} custom-call(bf16[32,2,8,256]{3,2,1,0:T(8,128)(2,1)} %copy-done.1, bf16[1,8,256]{2,1,0:T(8,128)(2,1)} %reshape.194.top_ref), custom_call_target="tpu_custom_call" | custom-call | tf_op jit(solution)/shard_map/cascade/pallas_call | solution.py:26
  35.3 5.1 %all-to-all-start.1 = ((bf16[32,8,256]{2,1,0:T(8,128)(2,1)}), bf16[32,8,256]{2,1,0:T(8,128)(2,1)S(1)}, u32[]{:S(2)}, u32[]{:S(2)}) async-start(bf16[32,8,256]{2,1,0:T(8,128)(2,1)} %cascade.1), calls=%async_computation.1 | async-start | bytes 262144 | tf_op jit(solution)/shard_map/all_to_all | solution.py:34
  40.4 6.6 %all-to-all-done.1 = bf16[32,8,256]{2,1,0:T(8,128)(2,1)S(1)} async-done(((bf16[32,8,256]{2,1,0:T(8,128)(2,1)}), bf16[32,8,256]{2,1,0:T(8,128)(2,1)S(1)}, u32[]{:S(2)}, u32[]{:S(2)}) %all-to-all-start.1) | async-done | bytes 131104 | tf_op jit(solution)/shard_map/all_to_all | solution.py:34
  47.0 0.1 copy.17
  47.1 0.2 fusion.18
  47.2 0.2 fusion.38
  47.5 0.3 fusion.3
  47.8 0.1 abs_reduce_fusion
  47.9 0.1 multiply_convert_fusion.3
  48.1 79.6 %all-gather.2 = f16[768,2048]{1,0:T(8,128)(2,1)S(1)} all-gather(f16[24,2048]{1,0:T(8,128)(2,1)S(1)} %fusion.26), channel_id=2, replica_groups=mesh['section'=32,'expert'=32] {'expert'}, dimensions={0}, use_global_device_ids=true | all-gather | bytes 3244032 | tf_op jit(solution)/shard_map/all_gather | solution.py:97
  127.9 0.7 add_convert_fusion
  128.6 0.3 fusion.5
  129.0 0.7 fusion.6
  129.7 0.7 fusion.7
  130.3 0.3 copy-done.3
  130.6 0.5 fusion.15
  131.1 1.5 %fusion.1 = bf16[1,224,2048]{2,1,0:T(8,128)(2,1)} fusion(f32[2048,224]{0,1:T(8,128)S(1)} %fusion.15, f16[32,24,2048]{2,1,0:T(8,128)(2,1)S(1)} %bitcast.103, f32[32,8]{1,0:T(8,128)S(1)} %get-tuple-element.10, bf16[1,2,256,224]{2,3,1,0:T(8,128)(2,1)S(1)} %copy-done.3), kind=kOutput, calls=%fused_computation.2 | convolution fusion | flops 237371392 | bytes 3932160 | tf_op jit(solution)/shard_map/dot_general | solution.py:119
  132.6 0.6 fusion.27
  133.3 0.7 maximum_bitcast_fusion
  (28 shorter events, 0.7 us)
Async XLA Ops:
  0.6 128.4 %copy-start = (bf16[1,224,2048]{2,1,0:T(8,128)(2,1)S(1)}, bf16[1,224,2048]{2,1,0:T(8,128)(2,1)}, u32[]{:S(2)}) copy-start(bf16[1,224,2048]{2,1,0:T(8,128)(2,1)} %param.13) | copy-start | bytes 2752516
  5.0 42.3 %copy-start.2 = (bf16[1,2,16,2048]{3,2,1,0:T(8,128)(2,1)S(1)}, bf16[1,2,16,2048]{3,2,1,0:T(8,128)(2,1)}, u32[]{:S(2)}) copy-start(bf16[1,2,16,2048]{3,2,1,0:T(8,128)(2,1)} %param.8) | copy-start | bytes 393220
  5.9 24.4 %all-to-all-start = ((bf16[32,2,8,256]{3,2,1,0:T(8,128)(2,1)}), bf16[32,2,8,256]{3,2,1,0:T(8,128)(2,1)S(1)}, u32[]{:S(2)}, u32[]{:S(2)}) async-start(bf16[32,2,8,256]{3,2,1,0:T(8,128)(2,1)} %pad_maximum_fusion), calls=%async_computation | async-start | bytes 524288 | tf_op jit(solution)/shard_map/all_to_all | solution.py:34
  30.3 0.7 copy-start.1
  35.3 11.7 %all-to-all-start.1 = ((bf16[32,8,256]{2,1,0:T(8,128)(2,1)}), bf16[32,8,256]{2,1,0:T(8,128)(2,1)S(1)}, u32[]{:S(2)}, u32[]{:S(2)}) async-start(bf16[32,8,256]{2,1,0:T(8,128)(2,1)} %cascade.1), calls=%async_computation.1 | async-start | bytes 262144 | tf_op jit(solution)/shard_map/all_to_all | solution.py:34
  129.7 0.9 copy-start.3

commit v2 on v1

--- a/solution.py
+++ b/solution.py
@@ -15,19 +15,205 @@
         out_ref[layer] = cot.astype(jnp.bfloat16)
         if layer:
             prod = ur_ref[layer, 0].astype(jnp.float32) * cot
-            half = prod[:, :128] + prod[:, 128:]
-            diff = jnp.sum(jnp.sum(half, axis=1, keepdims=True), axis=0, keepdims=True)
+            total = prod[:, :128] + prod[:, 128:]
+            for shift in (4, 2, 1):
+                total = total + pltpu.roll(total, shift, 0)
+            diff = jnp.sum(total, axis=1, keepdims=True)
             cot = cot + diff * ur_ref[layer, 1].astype(jnp.float32)
             cot = cot.astype(jnp.bfloat16).astype(jnp.float32)
 
 
 def cascade(pairs, top_token):
     count = pairs.shape[0]
+    vmem = pl.BlockSpec(memory_space=pltpu.VMEM)
     return pl.pallas_call(
         cascade_kernel,
         out_shape=jax.ShapeDtypeStruct((count, 8, 256), jnp.bfloat16),
+        in_specs=[vmem, vmem],
+        out_specs=vmem,
+        compiler_params=pltpu.CompilerParams(vmem_limit_bytes=8 << 20),
         name="cascade",
     )(pairs, top_token)
+
+
+def fetch_kernel(weight_ref, hidden_ref, _, weight_out, hidden_out, sems):
+    copies = [
+        pltpu.make_async_copy(weight_ref, weight_out, sems.at[0]),
+        pltpu.make_async_copy(hidden_ref, hidden_out, sems.at[1]),
+    ]
+    for copy in copies:
+        copy.start()
+    for copy in copies:
+        copy.wait()
+
+
+def fetch(weight, hidden, after):
+    vmem = pl.BlockSpec(memory_space=pltpu.VMEM)
+    return pl.pallas_call(
+        fetch_kernel,
+        out_shape=(
+            jax.ShapeDtypeStruct(weight.shape, weight.dtype),
+            jax.ShapeDtypeStruct(hidden.shape, hidden.dtype),
+        ),
+        in_specs=[pl.BlockSpec(memory_space=pl.ANY)] * 3,
+        out_specs=(vmem, vmem),
+        scratch_shapes=[pltpu.SemaphoreType.DMA((2,))],
+        compiler_params=pltpu.CompilerParams(vmem_limit_bytes=8 << 20),
+        cost_estimate=pl.CostEstimate(flops=1 << 21, transcendentals=0, bytes_accessed=1 << 21),
+        name="fetch",
+    )(weight, hidden, after)
+
+
+def in_pieces(value):
+    high = value.astype(jnp.bfloat16)
+    rest = value - high.astype(jnp.float32)
+    middle = rest.astype(jnp.bfloat16)
+    low = (rest - middle.astype(jnp.float32)).astype(jnp.bfloat16)
+    return jnp.concatenate([high, middle, low], axis=0)
+
+
+def dims(left, right):
+    return (((left,), (right,)), ((), ()))
+
+
+def prepare_kernel(
+    ids_hbm, router_hbm, inputs_hbm, outs_hbm,
+    pairs_ref, diff_ref,
+    ids_ref, router_ref, inputs_ref, outs_ref, wide_ref, sems,
+):
+    copies = [
+        pltpu.make_async_copy(far, near, sems.at[index])
+        for index, (far, near) in enumerate(
+            (
+                (ids_hbm, ids_ref),
+                (router_hbm, router_ref),
+                (inputs_hbm, inputs_ref),
+                (outs_hbm, outs_ref),
+            )
+        )
+    ]
+    for copy in copies:
+        copy.start()
+    for copy in copies:
+        copy.wait()
+    micro, _, tok = ids_ref.shape
+    experts = router_ref.shape[0]
+    pieces = in_pieces(router_ref[...])
+    for part in range(micro):
+        span = pl.ds(part * tok, tok)
+        expert = lax.broadcasted_iota(jnp.int32, (experts, tok), 0)
+        first, second = ids_ref[part, 0:1, :], ids_ref[part, 1:2, :]
+        sign = (expert == first).astype(jnp.float32) - (expert == second).astype(jnp.float32)
+        logits = lax.dot_general(
+            pieces, inputs_ref[span, :], dims(1, 1), preferred_element_type=jnp.float32
+        )
+        logits = logits[:experts] + logits[experts : 2 * experts] + logits[2 * experts :]
+        gate = jax.nn.sigmoid(jnp.sum(sign * logits, axis=0, keepdims=True))
+        slope = in_pieces(gate * (1.0 - gate))
+        spread = lax.dot_general(
+            slope,
+            jnp.ones((3, 128), jnp.bfloat16),
+            dims(0, 0),
+            preferred_element_type=jnp.float32,
+        )
+        sign = sign.astype(jnp.bfloat16)
+        step = lax.dot_general(
+            jnp.concatenate([sign, sign, sign], axis=0),
+            pieces,
+            dims(0, 0),
+            preferred_element_type=jnp.float32,
+        )
+        diff = outs_ref[part, :, 0, :].astype(jnp.float32) - outs_ref[part, :, 1, :].astype(jnp.float32)
+        diff_ref[span, :] = diff
+        scaled = diff * spread[:, :1]
+        chunk = wide_ref.shape[3]
+        for row in range(8):
+            columns = slice(row * chunk, (row + 1) * chunk)
+            wide_ref[span, 0, row, :] = scaled[:, columns]
+            wide_ref[span, 1, row, :] = step[:, columns]
+    pairs_ref[...] = wide_ref[...].astype(jnp.bfloat16)
+
+
+def prepare(chosen, router, inputs, outputs):
+    tokens, width = inputs.shape
+    pairs = (tokens, 2, 8, width // 8)
+    return pl.pallas_call(
+        prepare_kernel,
+        out_shape=(
+            jax.ShapeDtypeStruct(pairs, jnp.bfloat16),
+            jax.ShapeDtypeStruct((tokens, width), jnp.float32),
+        ),
+        in_specs=[pl.BlockSpec(memory_space=pltpu.HBM)] * 4,
+        scratch_shapes=[
+            *(pltpu.VMEM(value.shape, value.dtype) for value in (chosen, router, inputs, outputs)),
+            pltpu.VMEM(pairs, jnp.float32),
+            pltpu.SemaphoreType.DMA((4,)),
+        ],
+        name="prepare",
+    )(chosen, router, inputs, outputs)
+
+
+def finish_kernel(
+    slots_ref, weight_ref, hidden_ref, router_ref, grad_ref,
+    hidden_out, down_out, router_out, grad_out,
+    hidden_buf, down_buf, sems,
+):
+    copies = [
+        pltpu.make_async_copy(router_ref, router_out, sems.at[0]),
+        pltpu.make_async_copy(grad_ref, grad_out, sems.at[1]),
+    ]
+    for copy in copies:
+        copy.start()
+    micro = slots_ref.shape[0]
+    width = weight_ref.shape[1]
+    chunk = width // 4
+    for index in range(4):
+        span = pl.ds(index * chunk, chunk)
+        total = 0.0
+        for part in range(micro):
+            total = total + lax.dot_general(
+                hidden_ref[part], slots_ref[part, :, span], dims(1, 0),
+                preferred_element_type=jnp.float32,
+            )
+        down_buf[:, span] = total.astype(jnp.bfloat16)
+        copy = pltpu.make_async_copy(
+            down_buf.at[:, span], down_out.at[:, span], sems.at[2 + index]
+        )
+        copy.start()
+        copies.append(copy)
+    for part in range(micro):
+        hidden_buf[part] = lax.dot_general(
+            weight_ref[...], slots_ref[part], dims(1, 1), preferred_element_type=jnp.float32
+        ).astype(jnp.bfloat16)
+        copy = pltpu.make_async_copy(
+            hidden_buf.at[part], hidden_out.at[part], sems.at[6 + part]
+        )
+        copy.start()
+        copies.append(copy)
+    for copy in copies:
+        copy.wait()
+
+
+def finish(slots, weight, hidden, router_grad, input_grad):
+    vmem = pl.BlockSpec(memory_space=pltpu.VMEM)
+    anywhere = pl.BlockSpec(memory_space=pl.ANY)
+    shapes = [
+        jax.ShapeDtypeStruct(value.shape, value.dtype)
+        for value in (hidden, weight, router_grad, input_grad)
+    ]
+    return pl.pallas_call(
+        finish_kernel,
+        out_shape=tuple(shapes),
+        in_specs=[vmem] * 5,
+        out_specs=tuple([anywhere] * 4),
+        scratch_shapes=[
+            pltpu.VMEM(hidden.shape, hidden.dtype),
+            pltpu.VMEM(weight.shape, weight.dtype),
+            pltpu.SemaphoreType.DMA((6 + hidden.shape[0],)),
+        ],
+        compiler_params=pltpu.CompilerParams(vmem_limit_bytes=16 << 20),
+        name="finish",
+    )(slots, weight, hidden, router_grad, input_grad)
 
 
 def swap(value):
@@ -47,7 +233,6 @@
     groups = lax.axis_size("expert")
     capacity = tok // 2
     inputs = layer_input[0].reshape(tokens, width).astype(jnp.float32)
-    outputs = expert_out[0].reshape(tokens, 2, width)
     router = router_w[0]
     experts = router.shape[1]
     chosen = expert_ids[0].reshape(tokens, 2)
@@ -57,15 +242,19 @@
     sign = select[:, 0] - select[:, 1]
     gate = jax.nn.sigmoid(jnp.sum(sign * logits, axis=-1))
     slope = gate * (1.0 - gate)
-    out_diff = outputs[:, 0].astype(jnp.float32) - outputs[:, 1].astype(jnp.float32)
     step = lax.dot_general(sign, router, (((1,), (1,)), ((), ())), precision=HIGH)
 
-    pairs = jnp.stack(
-        [(slope[:, None] * out_diff).astype(jnp.bfloat16), step.astype(jnp.bfloat16)], axis=1
-    ).reshape(tokens, 2, 8, width // 8)
+    pairs, out_diff = prepare(
+        expert_ids[0].transpose(0, 2, 1),
+        router.T,
+        layer_input[0].reshape(tokens, width),
+        expert_out[0],
+    )
     mine = lax.axis_index("section")
     top_token = lax.dynamic_slice_in_dim(top_grad.reshape(tokens, width), mine, 1, 0)
-    cots = cascade(swap(pairs), top_token.reshape(1, 8, width // 8))
+    received_pairs = swap(pairs)
+    cots = cascade(received_pairs, top_token.reshape(1, 8, width // 8))
+    weight, saved_hidden = fetch(down_w[0], hidden[0].transpose(0, 2, 1), cots)
     cot = swap(cots).reshape(tokens, width).astype(jnp.float32)
 
     logit_diff = slope * jnp.sum(out_diff * cot, axis=-1)
@@ -104,28 +293,24 @@
 
     others = jnp.sum(received(micro * capacity, experts - 1), axis=0)
     router_sum = jnp.concatenate([-jnp.sum(others, axis=0, keepdims=True), others], axis=0)
-    router_grad = router_sum.T / (tokens * groups)
-
-    weight = down_w[0]
-    hidden_parts = []
-    down_acc = 0.0
-    for part in range(micro):
-        slots = received(part * capacity, capacity).astype(jnp.bfloat16).reshape(-1, width)
-        hidden_parts.append(
-            lax.dot_general(
-                weight, slots, (((1,), (1,)), ((), ())), preferred_element_type=jnp.float32
-            ).astype(jnp.bfloat16)
-        )
-        down_acc = down_acc + lax.dot_general(
-            hidden[0, part], slots, (((0,), (0,)), ((), ())), preferred_element_type=jnp.float32
-        )
-    hidden_grad = jnp.stack(hidden_parts).transpose(0, 2, 1)
-    down_grad = down_acc
+    slots = jnp.stack(
+        [
+            received(part * capacity, capacity).astype(jnp.bfloat16).reshape(-1, width)
+            for part in range(micro)
+        ]
+    )
+    hidden_grad, down_grad, router_grad, input_grad = finish(
+        slots,
+        weight,
+        saved_hidden,
+        router_sum / (tokens * groups),
+        input_grad,
+    )
     return (
         input_grad.reshape(1, micro, tok, width),
-        router_grad[None],
-        hidden_grad[None],
-        down_grad.astype(jnp.bfloat16)[None],
+        router_grad.T[None],
+        hidden_grad.transpose(0, 2, 1)[None],
+        down_grad[None],
     )
 
 

time: 134 us -> 128 us (0.955)
  Pallas kernels: 4.32 us -> 8.78 us
  matrix products: 6.14 us -> 2 us
  local copies, waits for them, and re-layouts: 4.77 us -> 1.3 us
  other arithmetic: 4 us -> 1.7 us
    pallas_call x0 -> x3, Pallas kernels: none -> 5.42 us  [the longest x1 2.84 us: prepare(): pl.pallas_call(prepare_kernel, out_shape=(jax.ShapeDtypeStruct(pairs, jnp...]
    dot_general x4 -> x0, matrix products: 3.31 us -> none  [the longest x2 2 us: per_device(): lax.dot_general(hidden[0, part], slots, (((0,), (0,)), ((), ())), preferr...]
    unnamed x13 -> x14, local copies, waits for them, and re-layouts: 2.93 us -> 0.8 us
    broadcast_in_dim x2 -> x0, other arithmetic: 1.36 us -> none  [the longest x1 0.71 us: per_device(): hidden_grad[None]]
  transfers between devices with their start and end apart: 2 -> 2, of which waited for: 2 -> 2; matrix products, arithmetic and copies ran while one was open for 1% -> 2% of each run, Pallas kernels for 0% -> 0%
where the time goes in v2:
time: 128 us
  blocking collectives  79.8 us (62%)
  starting transfers between devices  21.9 us (17%)
  waiting for transfers between devices  11.3 us (9%)
  Pallas kernels  8.78 us (7%)
  matrix products  2 us (2%)
  other arithmetic  1.7 us (1%)
  local copies, waits for them, and re-layouts  1.3 us (1%)
    all_gather x1, blocking collectives, per_device(): got = lax.all_gather(sent, 'expert', axis=0, tiled=False)  79.8 us
    all_to_all x2, starting transfers between devices, swap(): return lax.all_to_all(value, 'section', 0, 0, tiled=True)  21.9 us
    all_to_all x2, waiting for transfers between devices, swap(): return lax.all_to_all(value, 'section', 0, 0, tiled=True)  11.3 us
    pallas_call x1, Pallas kernels, cascade(): pl.pallas_call(cascade_kernel, out_shape=jax.ShapeDtypeStruct((count, 8,...  3.36 us
    pallas_call x1, Pallas kernels, prepare(): pl.pallas_call(prepare_kernel, out_shape=(jax.ShapeDtypeStruct(pairs, jnp...  2.84 us
  transfers between devices with their start and end apart: 2, of which 2 were waited for; matrix products, arithmetic and copies ran while one was open for 2% of the time, Pallas kernels for 0%

profile of v2, /device:TPU:2, one launch (start us, length us, event | category | flops | bytes accessed | tf_op | source)
XLA Modules:
  0.0 127.6 jit_solution(1532722637514133459)
XLA Ops:
  0.6 0.0 copy-start
  0.7 2.8 %prepare.1 = (bf16[32,2,8,256]{3,2,1,0:T(8,128)(2,1)}, f32[32,2048]{1,0:T(8,128)}) custom-call(s32[2,2,16]{2,1,0:T(2,128)} %bitcast.80, f32[8,2048]{1,0:T(8,128)} %bitcast.75, bf16[32,2048]{1,0:T(8,128)(2,1)} %bitcast.71, bf16[2,16,2,2048]{3,2,1,0:T(2,128)(2,1)} %bitcast.76), custom_call_target="tpu_custom_call" | custom-call | tf_op jit(solution)/shard_map/prepare/pallas_call | solution.py:140
  3.5 0.0 copy-start.3
  3.5 16.8 %all-to-all-start = ((bf16[32,2,8,256]{3,2,1,0:T(8,128)(2,1)}), bf16[32,2,8,256]{3,2,1,0:T(8,128)(2,1)S(1)}, u32[]{:S(2)}, u32[]{:S(2)}) async-start(bf16[32,2,8,256]{3,2,1,0:T(8,128)(2,1)} %get-tuple-element.12), calls=%async_computation | async-start | bytes 524288 | tf_op jit(solution)/shard_map/all_to_all | solution.py:220
  20.4 0.7 copy.12
  21.1 0.1 reshape_squeeze.7
  21.2 1.1 fusion.6
  22.4 0.1 add.53
  22.5 0.1 fusion.17
  22.6 0.1 multiply_reduce_fusion.1
  22.7 0.1 mul.106
  22.7 5.3 %all-to-all-done.ur_ref = bf16[32,2,8,256]{3,2,1,0:T(8,128)(2,1)S(1)} async-done(((bf16[32,2,8,256]{3,2,1,0:T(8,128)(2,1)}), bf16[32,2,8,256]{3,2,1,0:T(8,128)(2,1)S(1)}, u32[]{:S(2)}, u32[]{:S(2)}) %all-to-all-start) | async-done | bytes 262176 | tf_op jit(solution)/shard_map/all_to_all | solution.py:220
  28.0 3.4 %cascade.1._ = bf16[32,8,256]{2,1,0:T(8,128)(2,1)} custom-call(bf16[32,2,8,256]{3,2,1,0:T(8,128)(2,1)S(1)} %all-to-all-done.ur_ref, bf16[1,8,256]{2,1,0:T(8,128)(2,1)S(1)} %reshape.173.top_ref), custom_call_target="tpu_custom_call" | custom-call | tf_op jit(solution)/shard_map/cascade/pallas_call | solution.py:29
  31.4 5.1 %all-to-all-start.1 = ((bf16[32,8,256]{2,1,0:T(8,128)(2,1)}), bf16[32,8,256]{2,1,0:T(8,128)(2,1)S(1)}, u32[]{:S(2)}, u32[]{:S(2)}) async-start(bf16[32,8,256]{2,1,0:T(8,128)(2,1)} %cascade.1._), calls=%async_computation.1 | async-start | bytes 262144 | tf_op jit(solution)/shard_map/all_to_all | solution.py:220
  36.5 0.5 fetch.1
  37.1 6.0 %all-to-all-done.1 = bf16[32,8,256]{2,1,0:T(8,128)(2,1)S(1)} async-done(((bf16[32,8,256]{2,1,0:T(8,128)(2,1)}), bf16[32,8,256]{2,1,0:T(8,128)(2,1)S(1)}, u32[]{:S(2)}, u32[]{:S(2)}) %all-to-all-start.1) | async-done | bytes 131104 | tf_op jit(solution)/shard_map/all_to_all | solution.py:220
  43.1 0.1 copy.13
  43.2 0.1 multiply_reduce_fusion
  43.4 0.2 fusion.22
  43.6 0.1 reshape.175
  43.6 0.3 fusion.3
  43.9 0.0 copy-start.4
  43.9 0.1 abs_reduce_fusion
  44.1 0.1 multiply_convert_fusion.2
  44.2 79.8 %all-gather.2 = f16[768,2048]{1,0:T(8,128)(2,1)S(1)} all-gather(f16[24,2048]{1,0:T(8,128)(2,1)S(1)} %fusion.12), channel_id=2, replica_groups=mesh['section'=32,'expert'=32] {'expert'}, dimensions={0}, use_global_device_ids=true | all-gather | bytes 3244032 | tf_op jit(solution)/shard_map/all_gather | solution.py:286
  124.0 0.1 slice.58
  124.1 0.1 fusion.31
  124.2 0.4 fusion.1.grad_ref
  124.6 0.3 fusion.5
  125.0 0.4 fusion.7
  125.4 0.2 pad_maximum_fusion.slots_ref
  125.6 2.0 %finish.1 = (bf16[2,224,256]{2,1,0:T(8,128)(2,1)}, bf16[224,2048]{1,0:T(8,128)(2,1)}, f32[8,2048]{1,0:T(8,128)}, bf16[32,2048]{1,0:T(8,128)(2,1)}) custom-call(bf16[2,256,2048]{2,1,0:T(8,128)(2,1)S(1)} %pad_maximum_fusion.slots_ref, bf16[224,2048]{1,0:T(8,128)(2,1)S(1)} %get-tuple-element.14.weight_ref, ...), custom_call_target="tpu_custom_call" | custom-call | tf_op jit(solution)/shard_map/finish/pallas_call | solution.py:204
  (25 shorter events, 0.3 us)
Async XLA Ops:
  0.6 20.5 %copy-start = (bf16[2,16,2048]{2,1,0:T(8,128)(2,1)S(1)}, bf16[2,16,2048]{2,1,0:T(8,128)(2,1)}, u32[]{:S(2)}) copy-start(bf16[2,16,2048]{2,1,0:T(8,128)(2,1)} %param.7) | copy-start | bytes 393220
  0.6 35.9 %copy-start.1 = (bf16[1,224,2048]{2,1,0:T(8,128)(2,1)S(1)}, bf16[1,224,2048]{2,1,0:T(8,128)(2,1)}, u32[]{:S(2)}) copy-start(bf16[1,224,2048]{2,1,0:T(8,128)(2,1)} %param.13) | copy-start | bytes 2752516
  0.7 35.9 %copy-start.2 = (bf16[1,2,256,224]{2,3,1,0:T(8,128)(2,1)S(1)}, bf16[1,2,256,224]{2,3,1,0:T(8,128)(2,1)}, u32[]{:S(2)}) copy-start(bf16[1,2,256,224]{2,3,1,0:T(8,128)(2,1)} %param.12) | copy-start | bytes 688132
  3.5 39.7 %copy-start.5 = (f32[32,2048]{1,0:T(8,128)S(1)}, f32[32,2048]{1,0:T(8,128)}, u32[]{:S(2)}) copy-start(f32[32,2048]{1,0:T(8,128)} %get-tuple-element.13) | copy-start | bytes 786436
  3.5 39.9 %copy-start.3 = (bf16[1,2,16,2048]{3,2,1,0:T(8,128)(2,1)S(1)}, bf16[1,2,16,2048]{3,2,1,0:T(8,128)(2,1)}, u32[]{:S(2)}) copy-start(bf16[1,2,16,2048]{3,2,1,0:T(8,128)(2,1)} %param.8) | copy-start | bytes 393220
  3.5 24.5 %all-to-all-start = ((bf16[32,2,8,256]{3,2,1,0:T(8,128)(2,1)}), bf16[32,2,8,256]{3,2,1,0:T(8,128)(2,1)S(1)}, u32[]{:S(2)}, u32[]{:S(2)}) async-start(bf16[32,2,8,256]{3,2,1,0:T(8,128)(2,1)} %get-tuple-element.12), calls=%async_computation | async-start | bytes 524288 | tf_op jit(solution)/shard_map/all_to_all | solution.py:220
  31.4 11.7 %all-to-all-start.1 = ((bf16[32,8,256]{2,1,0:T(8,128)(2,1)}), bf16[32,8,256]{2,1,0:T(8,128)(2,1)S(1)}, u32[]{:S(2)}, u32[]{:S(2)}) async-start(bf16[32,8,256]{2,1,0:T(8,128)(2,1)} %cascade.1._), calls=%async_computation.1 | async-start | bytes 262144 | tf_op jit(solution)/shard_map/all_to_all | solution.py:220
  43.9 80.2 %copy-start.4 = (f32[1,2048,8]{1,2,0:T(8,128)S(1)}, f32[1,2048,8]{1,2,0:T(8,128)}, u32[]{:S(2)}) copy-start(f32[1,2048,8]{1,2,0:T(8,128)} %param.10) | copy-start | bytes 196612

commit v3 on v2

--- a/solution.py
+++ b/solution.py
@@ -8,19 +8,46 @@
 HIGH = lax.Precision.HIGHEST
 
 
+BLOCK = 4
+
+
+def spread_sum(prod):
+    total = prod[:, :128] + prod[:, 128:]
+    for shift in (4, 2, 1):
+        total = total + pltpu.roll(total, shift, 0)
+    return jnp.sum(total, axis=1, keepdims=True)
+
+
 def cascade_kernel(ur_ref, top_ref, out_ref):
     count = ur_ref.shape[0]
+
+    def scaled(layer):
+        return ur_ref[layer, 0].astype(jnp.float32)
+
+    def step(layer):
+        return ur_ref[layer, 1].astype(jnp.float32)
+
+    blocks = [
+        list(range(first, max(first - BLOCK, -1), -1)) for first in range(count - 1, -1, -BLOCK)
+    ]
+    cross = {
+        (low, high): spread_sum(scaled(low) * step(high))
+        for block in blocks
+        for high in block
+        for low in block
+        if 0 < low < high
+    }
     cot = top_ref[0].astype(jnp.float32)
-    for layer in reversed(range(count)):
-        out_ref[layer] = cot.astype(jnp.bfloat16)
-        if layer:
-            prod = ur_ref[layer, 0].astype(jnp.float32) * cot
-            total = prod[:, :128] + prod[:, 128:]
-            for shift in (4, 2, 1):
-                total = total + pltpu.roll(total, shift, 0)
-            diff = jnp.sum(total, axis=1, keepdims=True)
-            cot = cot + diff * ur_ref[layer, 1].astype(jnp.float32)
-            cot = cot.astype(jnp.bfloat16).astype(jnp.float32)
+    for block in blocks:
+        sums = {layer: spread_sum(scaled(layer) * cot) for layer in block if layer}
+        for layer in block:
+            out_ref[layer] = cot.astype(jnp.bfloat16)
+            if layer:
+                cot = cot + sums[layer] * step(layer)
+                cot = cot.astype(jnp.bfloat16).astype(jnp.float32)
+                for low in block:
+                    if 0 < low < layer:
+                        sums[low] = sums[low] + sums[layer] * cross[low, layer]
 
 
 def cascade(pairs, top_token):
@@ -164,15 +191,21 @@
     ]
     for copy in copies:
         copy.start()
-    micro = slots_ref.shape[0]
+    micro = hidden_ref.shape[0]
     width = weight_ref.shape[1]
+    capacity = slots_ref.shape[1] // micro
+
+    def slots(part, span):
+        value = slots_ref[:, part * capacity : (part + 1) * capacity, span]
+        return value.reshape(-1, value.shape[-1])
+
     chunk = width // 4
     for index in range(4):
-        span = pl.ds(index * chunk, chunk)
+        span = slice(index * chunk, (index + 1) * chunk)
         total = 0.0
         for part in range(micro):
             total = total + lax.dot_general(
-                hidden_ref[part], slots_ref[part, :, span], dims(1, 0),
+                hidden_ref[part], slots(part, span), dims(1, 0),
                 preferred_element_type=jnp.float32,
             )
         down_buf[:, span] = total.astype(jnp.bfloat16)
@@ -183,7 +216,8 @@
         copies.append(copy)
     for part in range(micro):
         hidden_buf[part] = lax.dot_general(
-            weight_ref[...], slots_ref[part], dims(1, 1), preferred_element_type=jnp.float32
+            weight_ref[...], slots(part, slice(None)), dims(1, 1),
+            preferred_element_type=jnp.float32,
         ).astype(jnp.bfloat16)
         copy = pltpu.make_async_copy(
             hidden_buf.at[part], hidden_out.at[part], sems.at[6 + part]
@@ -293,12 +327,7 @@
 
     others = jnp.sum(received(micro * capacity, experts - 1), axis=0)
     router_sum = jnp.concatenate([-jnp.sum(others, axis=0, keepdims=True), others], axis=0)
-    slots = jnp.stack(
-        [
-            received(part * capacity, capacity).astype(jnp.bfloat16).reshape(-1, width)
-            for part in range(micro)
-        ]
-    )
+    slots = received(0, micro * capacity).astype(jnp.bfloat16)
     hidden_grad, down_grad, router_grad, input_grad = finish(
         slots,
         weight,

time: 128 us -> 126 us (0.984)
  the two profiles are of different devices: /device:TPU:2 before, /device:TPU:8 now
where the time goes in v3:
time: 126 us; the launch traced here: 125 us
  blocking collectives  79.6 us (63%)
  starting transfers between devices  22 us (17%)
  waiting for transfers between devices  9.04 us (7%)
  Pallas kernels  6.79 us (5%)
  local copies, waits for them, and re-layouts  3.34 us (3%)
  matrix products  2 us (2%)
  other arithmetic  1.53 us (1%)
    all_gather x1, blocking collectives, per_device(): got = lax.all_gather(sent, 'expert', axis=0, tiled=False)  79.6 us
    all_to_all x2, starting transfers between devices, swap(): return lax.all_to_all(value, 'section', 0, 0, tiled=True)  22 us
    all_to_all x2, waiting for transfers between devices, swap(): return lax.all_to_all(value, 'section', 0, 0, tiled=True)  9.04 us
    unnamed x14, local copies, waits for them, and re-layouts  2.91 us
    pallas_call x1, Pallas kernels, prepare(): pl.pallas_call(prepare_kernel, out_shape=(jax.ShapeDtypeStruct(pairs, jnp...  2.8 us
  transfers between devices with their start and end apart: 2, of which 2 were waited for; matrix products, arithmetic and copies ran while one was open for 2% of the time, Pallas kernels for 0%

profile of v3, /device:TPU:8, one launch (start us, length us, event | category | flops | bytes accessed | tf_op | source)
XLA Modules:
  0.0 125.2 jit_solution(1610180580838667713)
XLA Ops:
  0.6 0.0 copy-start
  0.6 0.0 copy-start.3
  0.7 0.0 copy-start.4
  0.7 2.8 %prepare.1 = (bf16[32,2,8,256]{3,2,1,0:T(8,128)(2,1)}, f32[32,2048]{1,0:T(8,128)}) custom-call(s32[2,2,16]{2,1,0:T(2,128)} %bitcast.77, f32[8,2048]{1,0:T(8,128)} %bitcast.72, bf16[32,2048]{1,0:T(8,128)(2,1)} %bitcast.68, bf16[2,16,2,2048]{3,2,1,0:T(2,128)(2,1)} %bitcast.73), custom_call_target="tpu_custom_call" | custom-call | tf_op jit(solution)/shard_map/prepare/pallas_call | solution.py:167
  3.5 16.8 %all-to-all-start = ((bf16[32,2,8,256]{3,2,1,0:T(8,128)(2,1)}), bf16[32,2,8,256]{3,2,1,0:T(8,128)(2,1)S(1)}, u32[]{:S(2)}, u32[]{:S(2)}) async-start(bf16[32,2,8,256]{3,2,1,0:T(8,128)(2,1)} %get-tuple-element.12), calls=%async_computation | async-start | bytes 524288 | tf_op jit(solution)/shard_map/all_to_all | solution.py:254
  20.3 0.7 copy.12
  21.0 0.1 reshape_squeeze.7
  21.1 1.1 fusion.6
  22.3 0.1 add.53
  22.4 0.1 fusion.15
  22.5 0.1 multiply_reduce_fusion.1
  22.6 0.1 mul.98
  22.7 5.1 %all-to-all-done.ur_ref = bf16[32,2,8,256]{3,2,1,0:T(8,128)(2,1)S(1)} async-done(((bf16[32,2,8,256]{3,2,1,0:T(8,128)(2,1)}), bf16[32,2,8,256]{3,2,1,0:T(8,128)(2,1)S(1)}, u32[]{:S(2)}, u32[]{:S(2)}) %all-to-all-start) | async-done | bytes 262176 | tf_op jit(solution)/shard_map/all_to_all | solution.py:254
  27.8 1.4 %cascade.1._ = bf16[32,8,256]{2,1,0:T(8,128)(2,1)} custom-call(bf16[32,2,8,256]{3,2,1,0:T(8,128)(2,1)S(1)} %all-to-all-done.ur_ref, bf16[1,8,256]{2,1,0:T(8,128)(2,1)S(1)} %reshape.172.top_ref), custom_call_target="tpu_custom_call" | custom-call | tf_op jit(solution)/shard_map/cascade/pallas_call | solution.py:56
  29.2 5.2 %all-to-all-start.1 = ((bf16[32,8,256]{2,1,0:T(8,128)(2,1)}), bf16[32,8,256]{2,1,0:T(8,128)(2,1)S(1)}, u32[]{:S(2)}, u32[]{:S(2)}) async-start(bf16[32,8,256]{2,1,0:T(8,128)(2,1)} %cascade.1._), calls=%async_computation.1 | async-start | bytes 262144 | tf_op jit(solution)/shard_map/all_to_all | solution.py:254
  34.4 1.2 copy-done.1
  35.6 0.9 copy-done.2
  36.6 0.5 fetch.1
  37.1 3.9 %all-to-all-done.1 = bf16[32,8,256]{2,1,0:T(8,128)(2,1)S(1)} async-done(((bf16[32,8,256]{2,1,0:T(8,128)(2,1)}), bf16[32,8,256]{2,1,0:T(8,128)(2,1)S(1)}, u32[]{:S(2)}, u32[]{:S(2)}) %all-to-all-start.1) | async-done | bytes 131104 | tf_op jit(solution)/shard_map/all_to_all | solution.py:254
  41.0 0.1 copy.13
  41.1 0.1 multiply_reduce_fusion
  41.3 0.4 fusion.1.grad_ref
  41.7 0.2 fusion.20
  41.9 0.1 reshape.174
  42.0 0.3 fusion.3
  42.3 0.1 abs_reduce_fusion
  42.4 0.1 multiply_convert_fusion.1
  42.6 79.6 %all-gather.2 = f16[768,2048]{1,0:T(8,128)(2,1)S(1)} all-gather(f16[24,2048]{1,0:T(8,128)(2,1)S(1)} %fusion.10), channel_id=2, replica_groups=mesh['section'=32,'expert'=32] {'expert'}, dimensions={0}, use_global_device_ids=true | all-gather | bytes 3244032 | tf_op jit(solution)/shard_map/all_gather | solution.py:320
  122.2 0.1 slice.48
  122.3 0.3 fusion.5
  122.7 0.4 multiply_convert_fusion.slots_ref
  123.2 2.0 %finish.1 = (bf16[2,224,256]{2,1,0:T(8,128)(2,1)}, bf16[224,2048]{1,0:T(8,128)(2,1)}, f32[8,2048]{1,0:T(8,128)}, bf16[32,2048]{1,0:T(8,128)(2,1)}) custom-call(bf16[32,16,2048]{2,1,0:T(8,128)(2,1)S(1)} %multiply_convert_fusion.slots_ref, bf16[224,2048]{1,0:T(8,128)(2,1)S(1)} %get-tuple-element.14.weight_ref, ...), custom_call_target="tpu_custom_call" | custom-call | tf_op jit(solution)/shard_map/finish/pallas_call | solution.py:238
  (23 shorter events, 0.3 us)
Async XLA Ops:
  0.6 20.4 %copy-start = (bf16[2,16,2048]{2,1,0:T(8,128)(2,1)S(1)}, bf16[2,16,2048]{2,1,0:T(8,128)(2,1)}, u32[]{:S(2)}) copy-start(bf16[2,16,2048]{2,1,0:T(8,128)(2,1)} %param.7) | copy-start | bytes 393220
  0.6 41.1 %copy-start.3 = (bf16[1,2,16,2048]{3,2,1,0:T(8,128)(2,1)S(1)}, bf16[1,2,16,2048]{3,2,1,0:T(8,128)(2,1)}, u32[]{:S(2)}) copy-start(bf16[1,2,16,2048]{3,2,1,0:T(8,128)(2,1)} %param.8) | copy-start | bytes 393220
  0.7 40.6 %copy-start.4 = (f32[1,2048,8]{1,2,0:T(8,128)S(1)}, f32[1,2048,8]{1,2,0:T(8,128)}, u32[]{:S(2)}) copy-start(f32[1,2048,8]{1,2,0:T(8,128)} %param.10) | copy-start | bytes 196612
  3.5 37.6 %copy-start.5 = (f32[32,2048]{1,0:T(8,128)S(1)}, f32[32,2048]{1,0:T(8,128)}, u32[]{:S(2)}) copy-start(f32[32,2048]{1,0:T(8,128)} %get-tuple-element.13) | copy-start | bytes 786436
  3.5 24.3 %all-to-all-start = ((bf16[32,2,8,256]{3,2,1,0:T(8,128)(2,1)}), bf16[32,2,8,256]{3,2,1,0:T(8,128)(2,1)S(1)}, u32[]{:S(2)}, u32[]{:S(2)}) async-start(bf16[32,2,8,256]{3,2,1,0:T(8,128)(2,1)} %get-tuple-element.12), calls=%async_computation | async-start | bytes 524288 | tf_op jit(solution)/shard_map/all_to_all | solution.py:254
  29.2 11.8 %all-to-all-start.1 = ((bf16[32,8,256]{2,1,0:T(8,128)(2,1)}), bf16[32,8,256]{2,1,0:T(8,128)(2,1)S(1)}, u32[]{:S(2)}, u32[]{:S(2)}) async-start(bf16[32,8,256]{2,1,0:T(8,128)(2,1)} %cascade.1._), calls=%async_computation.1 | async-start | bytes 262144 | tf_op jit(solution)/shard_map/all_to_all | solution.py:254
  34.4 1.2 copy-start.1
  35.6 0.9 copy-start.2

commit v4 on v3

--- a/solution.py
+++ b/solution.py
@@ -91,12 +91,12 @@
     )(weight, hidden, after)
 
 
-def in_pieces(value):
+def in_pieces(value, axis=0):
     high = value.astype(jnp.bfloat16)
     rest = value - high.astype(jnp.float32)
     middle = rest.astype(jnp.bfloat16)
     low = (rest - middle.astype(jnp.float32)).astype(jnp.bfloat16)
-    return jnp.concatenate([high, middle, low], axis=0)
+    return jnp.concatenate([high, middle, low], axis=axis)
 
 
 def dims(left, right):
@@ -105,8 +105,8 @@
 
 def prepare_kernel(
     ids_hbm, router_hbm, inputs_hbm, outs_hbm,
-    pairs_ref, diff_ref,
-    ids_ref, router_ref, inputs_ref, outs_ref, wide_ref, sems,
+    pairs_hbm,
+    ids_ref, router_ref, inputs_ref, outs_ref, wide_ref, pairs_ref, sems,
 ):
     copies = [
         pltpu.make_async_copy(far, near, sems.at[index])
@@ -123,6 +123,7 @@
         copy.start()
     for copy in copies:
         copy.wait()
+    sent = []
     micro, _, tok = ids_ref.shape
     experts = router_ref.shape[0]
     pieces = in_pieces(router_ref[...])
@@ -151,14 +152,18 @@
             preferred_element_type=jnp.float32,
         )
         diff = outs_ref[part, :, 0, :].astype(jnp.float32) - outs_ref[part, :, 1, :].astype(jnp.float32)
-        diff_ref[span, :] = diff
         scaled = diff * spread[:, :1]
         chunk = wide_ref.shape[3]
         for row in range(8):
             columns = slice(row * chunk, (row + 1) * chunk)
             wide_ref[span, 0, row, :] = scaled[:, columns]
             wide_ref[span, 1, row, :] = step[:, columns]
-    pairs_ref[...] = wide_ref[...].astype(jnp.bfloat16)
+        pairs_ref[span] = wide_ref[span].astype(jnp.bfloat16)
+        copy = pltpu.make_async_copy(pairs_ref.at[span], pairs_hbm.at[span], sems.at[4 + part])
+        copy.start()
+        sent.append(copy)
+    for copy in sent:
+        copy.wait()
 
 
 def prepare(chosen, router, inputs, outputs):
@@ -166,18 +171,76 @@
     pairs = (tokens, 2, 8, width // 8)
     return pl.pallas_call(
         prepare_kernel,
-        out_shape=(
-            jax.ShapeDtypeStruct(pairs, jnp.bfloat16),
-            jax.ShapeDtypeStruct((tokens, width), jnp.float32),
-        ),
+        out_shape=jax.ShapeDtypeStruct(pairs, jnp.bfloat16),
         in_specs=[pl.BlockSpec(memory_space=pltpu.HBM)] * 4,
+        out_specs=pl.BlockSpec(memory_space=pltpu.HBM),
         scratch_shapes=[
             *(pltpu.VMEM(value.shape, value.dtype) for value in (chosen, router, inputs, outputs)),
             pltpu.VMEM(pairs, jnp.float32),
-            pltpu.SemaphoreType.DMA((4,)),
+            pltpu.VMEM(pairs, jnp.bfloat16),
+            pltpu.SemaphoreType.DMA((4 + chosen.shape[0],)),
         ],
         name="prepare",
     )(chosen, router, inputs, outputs)
+
+
+def middle_kernel(
+    cots_ref, outs_ref, inputs_ref, step_ref, sign_ref, slope_ref, pick_ref,
+    held_ref, grad_ref,
+    wide_ref,
+):
+    micro, tok = outs_ref.shape[:2]
+    capacity, experts = pick_ref.shape[1], sign_ref.shape[1]
+    count = micro * capacity
+    wide_ref[...] = cots_ref[...].astype(jnp.float32)
+    groups, router = [], 0.0
+    for part in range(micro):
+        span = pl.ds(part * tok, tok)
+        cot = jnp.concatenate([wide_ref[span, row, :] for row in range(8)], axis=1)
+        diff = outs_ref[part, :, 0, :].astype(jnp.float32) - outs_ref[part, :, 1, :].astype(jnp.float32)
+        change = slope_ref[span, :] * jnp.sum(diff * cot, axis=1, keepdims=True)
+        grad_ref[span, :] = (cot + change * step_ref[span, :]).astype(jnp.bfloat16)
+        rows = lax.dot_general(
+            in_pieces(pick_ref[part]), cot.astype(jnp.bfloat16), dims(1, 0),
+            preferred_element_type=jnp.float32,
+        )
+        rows = rows[:capacity] + rows[capacity : 2 * capacity] + rows[2 * capacity :]
+        groups.append(rows.astype(jnp.bfloat16).astype(jnp.float32))
+        parts = lax.dot_general(
+            in_pieces(change * sign_ref[span, :], 1), inputs_ref[span, :], dims(0, 0),
+            preferred_element_type=jnp.float32,
+        )
+        router = router + (parts[:experts] + parts[experts : 2 * experts] + parts[2 * experts :])
+    groups.append(router)
+    lane = lax.broadcasted_iota(jnp.int32, (capacity, 128), 1)
+    row = lax.broadcasted_iota(jnp.int32, (capacity, 128), 0)
+    powers = jnp.zeros((1, 128), jnp.float32)
+    for index, value in enumerate(groups):
+        peak = jnp.max(jnp.abs(value), axis=1, keepdims=True)
+        power = jnp.clip(jnp.ceil(jnp.log2(jnp.maximum(peak, 1e-30))), -100.0, 120.0)
+        held_ref[index * capacity : (index + 1) * capacity, :] = value * jnp.exp2(-power)
+        powers = powers + jnp.sum(
+            jnp.where(lane == row + index * capacity, power, 0.0), axis=0, keepdims=True
+        )
+    held_ref[count : count + 1, :] = jnp.zeros((1, held_ref.shape[1]), jnp.float32)
+    held_ref[count : count + 1, :128] = powers
+
+
+def middle(cots, outputs, inputs, step, sign, slope, pick):
+    vmem = pl.BlockSpec(memory_space=pltpu.VMEM)
+    rows = pick.shape[0] * pick.shape[1] + sign.shape[1]
+    return pl.pallas_call(
+        middle_kernel,
+        out_shape=(
+            jax.ShapeDtypeStruct((rows, inputs.shape[1]), jnp.float32),
+            jax.ShapeDtypeStruct(inputs.shape, jnp.bfloat16),
+        ),
+        in_specs=[vmem] * 7,
+        out_specs=(vmem, vmem),
+        scratch_shapes=[pltpu.VMEM(cots.shape, jnp.float32)],
+        compiler_params=pltpu.CompilerParams(vmem_limit_bytes=8 << 20),
+        name="middle",
+    )(cots, outputs, inputs, step, sign, slope, pick)
 
 
 def finish_kernel(
@@ -254,12 +317,6 @@
     return lax.all_to_all(value, "section", 0, 0, tiled=True)
 
 
-def to_half(value):
-    peak = jnp.max(jnp.abs(value), axis=-1, keepdims=True)
-    power = jnp.clip(jnp.ceil(jnp.log2(jnp.maximum(peak, 1e-30))), -100.0, 120.0)
-    return (value * jnp.exp2(-power)).astype(jnp.float16), power[..., 0]
-
-
 def per_device(top_grad, layer_input, expert_out, router_w, expert_ids, hidden, down_w):
     micro, tok, width = top_grad.shape
     tokens = micro * tok
@@ -278,7 +335,7 @@
     slope = gate * (1.0 - gate)
     step = lax.dot_general(sign, router, (((1,), (1,)), ((), ())), precision=HIGH)
 
-    pairs, out_diff = prepare(
+    pairs = prepare(
         expert_ids[0].transpose(0, 2, 1),
         router.T,
         layer_input[0].reshape(tokens, width),
@@ -289,15 +346,6 @@
     received_pairs = swap(pairs)
     cots = cascade(received_pairs, top_token.reshape(1, 8, width // 8))
     weight, saved_hidden = fetch(down_w[0], hidden[0].transpose(0, 2, 1), cots)
-    cot = swap(cots).reshape(tokens, width).astype(jnp.float32)
-
-    logit_diff = slope * jnp.sum(out_diff * cot, axis=-1)
-    input_grad = (cot + logit_diff[:, None] * step).astype(jnp.bfloat16)
-    logit_grad = logit_diff[:, None] * sign
-    router_part = lax.dot_general(
-        logit_grad[:, 1:], inputs, (((0,), (0,)), ((), ())), precision=HIGH
-    )
-
     is_zero = (chosen == 0).astype(jnp.float32)
     zero_gate = gate * is_zero[:, 0] + (1.0 - gate) * is_zero[:, 1]
     routed = (is_zero[:, 0] + is_zero[:, 1]).reshape(micro, tok)
@@ -307,27 +355,26 @@
     pick = ((slot_pos[:, None, :] == slot_ids[:, None]) & (routed[:, None, :] > 0.5)).astype(
         jnp.float32
     )
-    scaled = (zero_gate[:, None] * cot).reshape(micro, tok, width)
-    rows = jnp.einsum("mcu,mud->mcd", pick, scaled, precision=HIGH).astype(jnp.bfloat16)
-
-    held = jnp.concatenate(
-        [rows.reshape(micro * capacity, width).astype(jnp.float32), router_part], axis=0
-    )
-    half, power = to_half(held)
-    powers = jnp.zeros((1, width), jnp.float16)
-    powers = lax.dynamic_update_slice(powers, power[None].astype(jnp.float16), (0, 0))
-    sent = jnp.concatenate([half, powers], axis=0)
-    got = lax.all_gather(sent, "expert", axis=0, tiled=False)
-
-    scale = jnp.exp2(got[:, -1, : micro * capacity + experts - 1].astype(jnp.float32))
+    held, input_grad = middle(
+        swap(cots),
+        expert_out[0],
+        layer_input[0].reshape(tokens, width),
+        step,
+        sign,
+        slope[:, None],
+        pick * zero_gate.reshape(micro, 1, tok),
+    )
+    got = lax.all_gather(held.astype(jnp.float16), "expert", axis=0, tiled=False)
+    count = micro * capacity
+    scale = jnp.exp2(got[:, count, : count + experts].astype(jnp.float32))
 
     def received(first, size):
         part = got[:, first : first + size].astype(jnp.float32)
         return part * scale[:, first : first + size, None]
 
-    others = jnp.sum(received(micro * capacity, experts - 1), axis=0)
+    others = jnp.sum(received(count + 1, experts - 1), axis=0)
     router_sum = jnp.concatenate([-jnp.sum(others, axis=0, keepdims=True), others], axis=0)
-    slots = received(0, micro * capacity).astype(jnp.bfloat16)
+    slots = received(0, count).astype(jnp.bfloat16)
     hidden_grad, down_grad, router_grad, input_grad = finish(
         slots,
         weight,

time: 126 us -> 125 us (level)
  the two profiles are of different devices: /device:TPU:8 before, /device:TPU:2 now
where the time goes in v4:
time: 125 us
  blocking collectives  79.9 us (64%)
  starting transfers between devices  21.8 us (17%)
  waiting for transfers between devices  8.79 us (7%)
  Pallas kernels  7.57 us (6%)
  matrix products  2.44 us (2%)
  local copies, waits for them, and re-layouts  2.21 us (2%)
  other arithmetic  1.25 us (1%)
    all_gather x1, blocking collectives, per_device(): lax.all_gather(held.astype(jnp.float16), 'expert', axis=0, tiled=False)  79.9 us
    all_to_all x2, starting transfers between devices, swap(): return lax.all_to_all(value, 'section', 0, 0, tiled=True)  21.8 us
    all_to_all x2, waiting for transfers between devices, swap(): return lax.all_to_all(value, 'section', 0, 0, tiled=True)  8.79 us
    pallas_call x1, Pallas kernels, prepare(): pl.pallas_call(prepare_kernel, out_shape=jax.ShapeDtypeStruct(pairs, jnp....  2.77 us
  transfers between devices with their start and end apart: 2, of which 2 were waited for; matrix products, arithmetic and copies ran while one was open for 3% of the time, Pallas kernels for 0%

profile of v4, /device:TPU:2, one launch (start us, length us, event | category | flops | bytes accessed | tf_op | source)
XLA Modules:
  0.0 124.7 jit_solution(8643526907548547457)
XLA Ops:
  0.6 0.0 copy-start
  0.6 0.0 copy-start.1
  0.7 0.0 copy-start.2
  0.7 0.0 copy-start.3
  0.7 2.8 %prepare.1 = bf16[32,2,8,256]{3,2,1,0:T(8,128)(2,1)} custom-call(s32[2,2,16]{2,1,0:T(2,128)} %bitcast.52, f32[8,2048]{1,0:T(8,128)} %bitcast.48, bf16[32,2048]{1,0:T(8,128)(2,1)} %bitcast.38, bf16[2,16,2,2048]{3,2,1,0:T(2,128)(2,1)} %bitcast.41), custom_call_target="tpu_custom_call" | custom-call | tf_op jit(solution)/shard_map/prepare/pallas_call | solution.py:172
  3.5 16.7 %all-to-all-start = ((bf16[32,2,8,256]{3,2,1,0:T(8,128)(2,1)}), bf16[32,2,8,256]{3,2,1,0:T(8,128)(2,1)S(1)}, u32[]{:S(2)}, u32[]{:S(2)}) async-start(bf16[32,2,8,256]{3,2,1,0:T(8,128)(2,1)} %prepare.1), calls=%async_computation | async-start | bytes 524288 | tf_op jit(solution)/shard_map/all_to_all | solution.py:317
  20.2 0.7 copy.19
  20.8 0.1 eq.34
  20.9 0.1 fusion.6
  21.0 1.3 %fusion.2 = f32[32]{0:T(128)S(1)} fusion(f32[32,8]{1,0:T(8,128)S(1)} %fusion.9.sign_ref, bf16[32,2048]{1,0:T(8,128)(2,1)} %bitcast.39, f32[1,2048,8]{1,2,0:T(8,128)} %param.10), kind=kOutput, calls=%fused_computation.5 | convolution fusion | flops 6291936 | bytes 197760 | tf_op jit(solution)/shard_map/dot_general | solution.py:331
  22.3 0.1 div.28
  22.4 0.1 squeeze.30
  22.5 0.1 squeeze.31
  22.6 0.1 fusion.10
  22.7 0.1 copy.23
  22.8 0.1 multiply_reduce_fusion
  22.9 0.0 copy-done
  22.9 1.2 fusion.3.step_ref
  24.1 3.7 %all-to-all-done.ur_ref = bf16[32,2,8,256]{3,2,1,0:T(8,128)(2,1)S(1)} async-done(((bf16[32,2,8,256]{3,2,1,0:T(8,128)(2,1)}), bf16[32,2,8,256]{3,2,1,0:T(8,128)(2,1)S(1)}, u32[]{:S(2)}, u32[]{:S(2)}) %all-to-all-start) | async-done | bytes 262176 | tf_op jit(solution)/shard_map/all_to_all | solution.py:317
  27.8 1.4 %cascade.1._ = bf16[32,8,256]{2,1,0:T(8,128)(2,1)} custom-call(bf16[32,2,8,256]{3,2,1,0:T(8,128)(2,1)S(1)} %all-to-all-done.ur_ref, bf16[1,8,256]{2,1,0:T(8,128)(2,1)S(1)} %reshape.128.top_ref), custom_call_target="tpu_custom_call" | custom-call | tf_op jit(solution)/shard_map/cascade/pallas_call | solution.py:56
  29.3 5.1 %all-to-all-start.1 = ((bf16[32,8,256]{2,1,0:T(8,128)(2,1)}), bf16[32,8,256]{2,1,0:T(8,128)(2,1)S(1)}, u32[]{:S(2)}, u32[]{:S(2)}) async-start(bf16[32,8,256]{2,1,0:T(8,128)(2,1)} %cascade.1._), calls=%async_computation.1 | async-start | bytes 262144 | tf_op jit(solution)/shard_map/all_to_all | solution.py:317
  34.4 0.0 copy-start.4
  34.4 0.9 copy-done.4
  35.3 0.5 fetch.1
  35.8 5.1 %all-to-all-done.1.cots_ref = bf16[32,8,256]{2,1,0:T(8,128)(2,1)S(1)} async-done(((bf16[32,8,256]{2,1,0:T(8,128)(2,1)}), bf16[32,8,256]{2,1,0:T(8,128)(2,1)S(1)}, u32[]{:S(2)}, u32[]{:S(2)}) %all-to-all-start.1) | async-done | bytes 131104 | tf_op jit(solution)/shard_map/all_to_all | solution.py:317
  40.9 0.0 copy-done.1
  40.9 0.8 middle.1
  41.8 79.9 %all-gather.2 = f16[768,2048]{1,0:T(8,128)(2,1)S(1)} all-gather(f16[24,2048]{1,0:T(8,128)(2,1)S(1)} %convert_element_type.34), channel_id=2, replica_groups=mesh['section'=32,'expert'=32] {'expert'}, dimensions={0}, use_global_device_ids=true | all-gather | bytes 3244032 | tf_op jit(solution)/shard_map/all_gather | solution.py:367
  121.7 0.1 slice.44
  121.8 0.4 fusion.1
  122.2 0.4 multiply_convert_fusion.slots_ref
  122.7 2.0 %finish.1 = (bf16[2,224,256]{2,1,0:T(8,128)(2,1)}, bf16[224,2048]{1,0:T(8,128)(2,1)}, f32[8,2048]{1,0:T(8,128)}, bf16[32,2048]{1,0:T(8,128)(2,1)}) custom-call(bf16[32,16,2048]{2,1,0:T(8,128)(2,1)S(1)} %multiply_convert_fusion.slots_ref, bf16[224,2048]{1,0:T(8,128)(2,1)S(1)} %get-tuple-element.13.weight_ref, ...), custom_call_target="tpu_custom_call" | custom-call | tf_op jit(solution)/shard_map/finish/pallas_call | solution.py:301
  (19 shorter events, 0.2 us)
Async XLA Ops:
  0.6 22.3 %copy-start = (bf16[2,16,2048]{2,1,0:T(8,128)(2,1)S(1)}, bf16[2,16,2048]{2,1,0:T(8,128)(2,1)}, u32[]{:S(2)}) copy-start(bf16[2,16,2048]{2,1,0:T(8,128)(2,1)} %param.7) | copy-start | bytes 393220
  0.6 40.3 %copy-start.1 = (bf16[1,2,16,2048]{3,2,1,0:T(8,128)(2,1)S(1)}, bf16[1,2,16,2048]{3,2,1,0:T(8,128)(2,1)}, u32[]{:S(2)}) copy-start(bf16[1,2,16,2048]{3,2,1,0:T(8,128)(2,1)} %param.8) | copy-start | bytes 393220
  0.7 40.3 %copy-start.2 = (bf16[1,2,16,2,2048]{4,3,2,1,0:T(2,128)(2,1)S(1)}, bf16[1,2,16,2,2048]{4,3,2,1,0:T(2,128)(2,1)}, u32[]{:S(2)}) copy-start(bf16[1,2,16,2,2048]{4,3,2,1,0:T(2,128)(2,1)} %param.9) | copy-start | bytes 786436
  0.7 33.7 %copy-start.3 = (bf16[1,224,2048]{2,1,0:T(8,128)(2,1)S(1)}, bf16[1,224,2048]{2,1,0:T(8,128)(2,1)}, u32[]{:S(2)}) copy-start(bf16[1,224,2048]{2,1,0:T(8,128)(2,1)} %param.13) | copy-start | bytes 2752516
  3.5 24.4 %all-to-all-start = ((bf16[32,2,8,256]{3,2,1,0:T(8,128)(2,1)}), bf16[32,2,8,256]{3,2,1,0:T(8,128)(2,1)S(1)}, u32[]{:S(2)}, u32[]{:S(2)}) async-start(bf16[32,2,8,256]{3,2,1,0:T(8,128)(2,1)} %prepare.1), calls=%async_computation | async-start | bytes 524288 | tf_op jit(solution)/shard_map/all_to_all | solution.py:317
  29.3 11.7 %all-to-all-start.1 = ((bf16[32,8,256]{2,1,0:T(8,128)(2,1)}), bf16[32,8,256]{2,1,0:T(8,128)(2,1)S(1)}, u32[]{:S(2)}, u32[]{:S(2)}) async-start(bf16[32,8,256]{2,1,0:T(8,128)(2,1)} %cascade.1._), calls=%async_computation.1 | async-start | bytes 262144 | tf_op jit(solution)/shard_map/all_to_all | solution.py:317
  34.4 0.9 copy-start.4

commit v5 on v4

--- a/solution.py
+++ b/solution.py
@@ -18,7 +18,7 @@
     return jnp.sum(total, axis=1, keepdims=True)
 
 
-def cascade_kernel(ur_ref, top_ref, out_ref):
+def cascade_kernel(ur_ref, top_ref, _pick, _slope, _step, _weight, out_ref):
     count = ur_ref.shape[0]
 
     def scaled(layer):
@@ -50,20 +50,20 @@
                         sums[low] = sums[low] + sums[layer] * cross[low, layer]
 
 
-def cascade(pairs, top_token):
+def cascade(pairs, top_token, before):
     count = pairs.shape[0]
     vmem = pl.BlockSpec(memory_space=pltpu.VMEM)
     return pl.pallas_call(
         cascade_kernel,
         out_shape=jax.ShapeDtypeStruct((count, 8, 256), jnp.bfloat16),
-        in_specs=[vmem, vmem],
+        in_specs=[vmem] * 6,
         out_specs=vmem,
         compiler_params=pltpu.CompilerParams(vmem_limit_bytes=8 << 20),
         name="cascade",
-    )(pairs, top_token)
-
-
-def fetch_kernel(weight_ref, hidden_ref, _, weight_out, hidden_out, sems):
+    )(pairs, top_token, *before)
+
+
+def fetch_kernel(weight_ref, hidden_ref, weight_out, hidden_out, sems):
     copies = [
         pltpu.make_async_copy(weight_ref, weight_out, sems.at[0]),
         pltpu.make_async_copy(hidden_ref, hidden_out, sems.at[1]),
@@ -74,7 +74,7 @@
         copy.wait()
 
 
-def fetch(weight, hidden, after):
+def fetch(weight, hidden):
     vmem = pl.BlockSpec(memory_space=pltpu.VMEM)
     return pl.pallas_call(
         fetch_kernel,
@@ -82,13 +82,13 @@
             jax.ShapeDtypeStruct(weight.shape, weight.dtype),
             jax.ShapeDtypeStruct(hidden.shape, hidden.dtype),
         ),
-        in_specs=[pl.BlockSpec(memory_space=pl.ANY)] * 3,
+        in_specs=[pl.BlockSpec(memory_space=pl.ANY)] * 2,
         out_specs=(vmem, vmem),
         scratch_shapes=[pltpu.SemaphoreType.DMA((2,))],
         compiler_params=pltpu.CompilerParams(vmem_limit_bytes=8 << 20),
         cost_estimate=pl.CostEstimate(flops=1 << 21, transcendentals=0, bytes_accessed=1 << 21),
         name="fetch",
-    )(weight, hidden, after)
+    )(weight, hidden)
 
 
 def in_pieces(value, axis=0):
@@ -344,8 +344,7 @@
     mine = lax.axis_index("section")
     top_token = lax.dynamic_slice_in_dim(top_grad.reshape(tokens, width), mine, 1, 0)
     received_pairs = swap(pairs)
-    cots = cascade(received_pairs, top_token.reshape(1, 8, width // 8))
-    weight, saved_hidden = fetch(down_w[0], hidden[0].transpose(0, 2, 1), cots)
+    weight, saved_hidden = fetch(down_w[0], hidden[0].transpose(0, 2, 1))
     is_zero = (chosen == 0).astype(jnp.float32)
     zero_gate = gate * is_zero[:, 0] + (1.0 - gate) * is_zero[:, 1]
     routed = (is_zero[:, 0] + is_zero[:, 1]).reshape(micro, tok)
@@ -355,14 +354,17 @@
     pick = ((slot_pos[:, None, :] == slot_ids[:, None]) & (routed[:, None, :] > 0.5)).astype(
         jnp.float32
     )
+    pick = pick * zero_gate.reshape(micro, 1, tok)
+    before = (pick, slope[:, None], step, weight)
+    cots = cascade(received_pairs, top_token.reshape(1, 8, width // 8), before)
     held, input_grad = middle(
         swap(cots),
         expert_out[0],
         layer_input[0].reshape(tokens, width),
         step,
         sign,
-        slope[:, None],
-        pick * zero_gate.reshape(micro, 1, tok),
+        before[1],
+        pick,
     )
     got = lax.all_gather(held.astype(jnp.float16), "expert", axis=0, tiled=False)
     count = micro * capacity

time: 125 us -> 126 us (level)
  blocking collectives: 79.9 us -> 92.7 us
  waiting for transfers between devices: 8.79 us -> 0.98 us
  starting transfers between devices: 21.8 us -> 16.7 us
    all_to_all x0 -> x1, blocking collectives: none -> 12.9 us  [swap(): return lax.all_to_all(value, 'section', 0, 0, tiled=True)]
    all_to_all x2 -> x1, waiting for transfers between devices: 8.79 us -> 0.98 us  [swap(): return lax.all_to_all(value, 'section', 0, 0, tiled=True)]
    all_to_all x2 -> x1, starting transfers between devices: 21.8 us -> 16.7 us  [swap(): return lax.all_to_all(value, 'section', 0, 0, tiled=True)]
  transfers between devices with their start and end apart: 2 -> 1, of which waited for: 2 -> 1; matrix products, arithmetic and copies ran while one was open for 3% -> 3% of each run, Pallas kernels for 0% -> 0%
where the time goes in v5:
time: 126 us; the launch traced here: 125 us
  blocking collectives  92.7 us (74%)
  starting transfers between devices  16.7 us (13%)
  Pallas kernels  6.87 us (5%)
  local copies, waits for them, and re-layouts  3.39 us (3%)
  matrix products  2.45 us (2%)
    all_gather x1, blocking collectives, per_device(): lax.all_gather(held.astype(jnp.float16), 'expert', axis=0, tiled=False)  79.8 us
    all_to_all x1, starting transfers between devices, swap(): return lax.all_to_all(value, 'section', 0, 0, tiled=True)  16.7 us
    all_to_all x1, blocking collectives, swap(): return lax.all_to_all(value, 'section', 0, 0, tiled=True)  12.9 us
    unnamed x11, local copies, waits for them, and re-layouts  2.82 us
    pallas_call x1, Pallas kernels, prepare(): pl.pallas_call(prepare_kernel, out_shape=jax.ShapeDtypeStruct(pairs, jnp....  2.71 us
  transfers between devices with their start and end apart: 1, of which 1 were waited for; matrix products, arithmetic and copies ran while one was open for 3% of the time, Pallas kernels for 0%

profile of v5, /device:TPU:2, one launch (start us, length us, event | category | flops | bytes accessed | tf_op | source)
XLA Modules:
  0.0 125.2 jit_solution(10003691779885501408)
XLA Ops:
  0.6 0.0 copy-start
  0.6 0.0 copy-start.1
  0.7 0.0 copy-start.2
  0.7 2.7 %prepare.1 = bf16[32,2,8,256]{3,2,1,0:T(8,128)(2,1)} custom-call(s32[2,2,16]{2,1,0:T(2,128)} %bitcast.52, f32[8,2048]{1,0:T(8,128)} %bitcast.48, bf16[32,2048]{1,0:T(8,128)(2,1)} %bitcast.38, bf16[2,16,2,2048]{3,2,1,0:T(2,128)(2,1)} %bitcast.41), custom_call_target="tpu_custom_call" | custom-call | tf_op jit(solution)/shard_map/prepare/pallas_call | solution.py:172
  3.4 16.7 %all-to-all-start = ((bf16[32,2,8,256]{3,2,1,0:T(8,128)(2,1)}), bf16[32,2,8,256]{3,2,1,0:T(8,128)(2,1)S(1)}, u32[]{:S(2)}, u32[]{:S(2)}) async-start(bf16[32,2,8,256]{3,2,1,0:T(8,128)(2,1)} %prepare.1), calls=%async_computation | async-start | bytes 524288 | tf_op jit(solution)/shard_map/all_to_all | solution.py:317
  20.1 0.7 copy.19
  20.8 0.1 reshape_squeeze.9
  20.9 0.1 fusion.6
  21.0 1.3 %fusion.2 = f32[32]{0:T(128)S(1)} fusion(f32[32,8]{1,0:T(8,128)S(1)} %fusion.9.sign_ref, bf16[32,2048]{1,0:T(8,128)(2,1)} %bitcast.39, f32[1,2048,8]{1,2,0:T(8,128)} %param.10), kind=kOutput, calls=%fused_computation.5 | convolution fusion | flops 6291936 | bytes 197760 | tf_op jit(solution)/shard_map/dot_general | solution.py:331
  22.3 0.1 div.27
  22.4 0.1 squeeze.30
  22.5 0.1 squeeze.31
  22.6 0.1 fusion.10
  22.6 0.1 multiply_reduce_fusion
  22.7 0.1 copy.23
  22.9 0.0 copy-done
  22.9 0.0 copy-start.3
  22.9 1.2 copy-done.3
  24.1 0.9 copy-done.4
  25.0 0.5 fetch.1
  25.6 1.2 fusion.4._step.step_ref
  26.8 1.0 all-to-all-done.ur_ref
  27.8 0.8 cascade.1
  28.5 12.9 %all_to_all.10.cots_ref = bf16[32,8,256]{2,1,0:T(8,128)(2,1)S(1)} all-to-all(bf16[32,8,256]{2,1,0:T(8,128)(2,1)S(1)} %cascade.1), channel_id=1, replica_groups=mesh['section'=32,'expert'=32] {'section'}, dimensions={0} | all-to-all | bytes 262144 | tf_op jit(solution)/shard_map/all_to_all | solution.py:317
  41.4 0.0 copy-done.1
  41.4 0.0 copy-done.2
  41.4 0.8 middle.1
  42.3 79.8 %all-gather.2 = f16[768,2048]{1,0:T(8,128)(2,1)S(1)} all-gather(f16[24,2048]{1,0:T(8,128)(2,1)S(1)} %convert_element_type.34), channel_id=2, replica_groups=mesh['section'=32,'expert'=32] {'expert'}, dimensions={0}, use_global_device_ids=true | all-gather | bytes 3244032 | tf_op jit(solution)/shard_map/all_gather | solution.py:369
  122.1 0.1 slice.44
  122.2 0.4 fusion.1
  122.7 0.4 multiply_convert_fusion.slots_ref
  123.1 2.0 %finish.1 = (bf16[2,224,256]{2,1,0:T(8,128)(2,1)}, bf16[224,2048]{1,0:T(8,128)(2,1)}, f32[8,2048]{1,0:T(8,128)}, bf16[32,2048]{1,0:T(8,128)(2,1)}) custom-call(bf16[32,16,2048]{2,1,0:T(8,128)(2,1)S(1)} %multiply_convert_fusion.slots_ref, bf16[224,2048]{1,0:T(8,128)(2,1)S(1)} %get-tuple-element.12._weight.weight_ref, ...), custom_call_target="tpu_custom_call" | custom-call | tf_op jit(solution)/shard_map/finish/pallas_call | solution.py:301
  (18 shorter events, 0.2 us)
Async XLA Ops:
  0.6 22.2 %copy-start = (bf16[2,16,2048]{2,1,0:T(8,128)(2,1)S(1)}, bf16[2,16,2048]{2,1,0:T(8,128)(2,1)}, u32[]{:S(2)}) copy-start(bf16[2,16,2048]{2,1,0:T(8,128)(2,1)} %param.7) | copy-start | bytes 393220
  0.6 40.8 %copy-start.1 = (bf16[1,2,16,2048]{3,2,1,0:T(8,128)(2,1)S(1)}, bf16[1,2,16,2048]{3,2,1,0:T(8,128)(2,1)}, u32[]{:S(2)}) copy-start(bf16[1,2,16,2048]{3,2,1,0:T(8,128)(2,1)} %param.8) | copy-start | bytes 393220
  0.7 40.8 %copy-start.2 = (bf16[1,2,16,2,2048]{4,3,2,1,0:T(2,128)(2,1)S(1)}, bf16[1,2,16,2,2048]{4,3,2,1,0:T(2,128)(2,1)}, u32[]{:S(2)}) copy-start(bf16[1,2,16,2,2048]{4,3,2,1,0:T(2,128)(2,1)} %param.9) | copy-start | bytes 786436
  3.4 24.4 %all-to-all-start = ((bf16[32,2,8,256]{3,2,1,0:T(8,128)(2,1)}), bf16[32,2,8,256]{3,2,1,0:T(8,128)(2,1)S(1)}, u32[]{:S(2)}, u32[]{:S(2)}) async-start(bf16[32,2,8,256]{3,2,1,0:T(8,128)(2,1)} %prepare.1), calls=%async_computation | async-start | bytes 524288 | tf_op jit(solution)/shard_map/all_to_all | solution.py:317
  22.9 1.2 copy-start.3
  24.1 0.9 copy-start.4

commit v6 on v4

--- a/solution.py
+++ b/solution.py
@@ -8,7 +8,7 @@
 HIGH = lax.Precision.HIGHEST
 
 
-BLOCK = 4
+BLOCK = 8
 
 
 def spread_sum(prod):
@@ -121,12 +121,14 @@
     ]
     for copy in copies:
         copy.start()
-    for copy in copies:
+    for copy in copies[:2]:
         copy.wait()
-    sent = []
+    sent, spreads = [], []
     micro, _, tok = ids_ref.shape
     experts = router_ref.shape[0]
     pieces = in_pieces(router_ref[...])
+    chunk = wide_ref.shape[3]
+    copies[2].wait()
     for part in range(micro):
         span = pl.ds(part * tok, tok)
         expert = lax.broadcasted_iota(jnp.int32, (experts, tok), 0)
@@ -151,13 +153,16 @@
             dims(0, 0),
             preferred_element_type=jnp.float32,
         )
+        spreads.append(spread[:, :1])
+        for row in range(8):
+            wide_ref[span, 1, row, :] = step[:, row * chunk : (row + 1) * chunk]
+    copies[3].wait()
+    for part in range(micro):
+        span = pl.ds(part * tok, tok)
         diff = outs_ref[part, :, 0, :].astype(jnp.float32) - outs_ref[part, :, 1, :].astype(jnp.float32)
-        scaled = diff * spread[:, :1]
-        chunk = wide_ref.shape[3]
+        scaled = diff * spreads[part]
         for row in range(8):
-            columns = slice(row * chunk, (row + 1) * chunk)
-            wide_ref[span, 0, row, :] = scaled[:, columns]
-            wide_ref[span, 1, row, :] = step[:, columns]
+            wide_ref[span, 0, row, :] = scaled[:, row * chunk : (row + 1) * chunk]
         pairs_ref[span] = wide_ref[span].astype(jnp.bfloat16)
         copy = pltpu.make_async_copy(pairs_ref.at[span], pairs_hbm.at[span], sems.at[4 + part])
         copy.start()

time: 125 us -> 125 us (level)
  no operation moved by 1% of the time
where the time goes in v6:
time: 125 us
  blocking collectives  79.9 us (64%)
  starting transfers between devices  21.8 us (17%)
  waiting for transfers between devices  8.79 us (7%)
  Pallas kernels  7.31 us (6%)
  matrix products  2.44 us (2%)
  local copies, waits for them, and re-layouts  2.21 us (2%)
  other arithmetic  1.25 us (1%)
    all_gather x1, blocking collectives, per_device(): lax.all_gather(held.astype(jnp.float16), 'expert', axis=0, tiled=False)  79.9 us
    all_to_all x2, starting transfers between devices, swap(): return lax.all_to_all(value, 'section', 0, 0, tiled=True)  21.8 us
    all_to_all x2, waiting for transfers between devices, swap(): return lax.all_to_all(value, 'section', 0, 0, tiled=True)  8.79 us
    pallas_call x1, Pallas kernels, prepare(): pl.pallas_call(prepare_kernel, out_shape=jax.ShapeDtypeStruct(pairs, jnp....  2.81 us
  transfers between devices with their start and end apart: 2, of which 2 were waited for; matrix products, arithmetic and copies ran while one was open for 3% of the time, Pallas kernels for 0%

profile of v6, /device:TPU:2, one launch (start us, length us, event | category | flops | bytes accessed | tf_op | source)
XLA Modules:
  0.0 124.5 jit_solution(8579832656448591347)
XLA Ops:
  0.6 0.0 copy-start
  0.6 0.0 copy-start.1
  0.7 0.0 copy-start.2
  0.7 0.0 copy-start.3
  0.7 2.8 %prepare.1 = bf16[32,2,8,256]{3,2,1,0:T(8,128)(2,1)} custom-call(s32[2,2,16]{2,1,0:T(2,128)} %bitcast.52, f32[8,2048]{1,0:T(8,128)} %bitcast.48, bf16[32,2048]{1,0:T(8,128)(2,1)} %bitcast.38, bf16[2,16,2,2048]{3,2,1,0:T(2,128)(2,1)} %bitcast.41), custom_call_target="tpu_custom_call" | custom-call | tf_op jit(solution)/shard_map/prepare/pallas_call | solution.py:177
  3.5 16.7 %all-to-all-start = ((bf16[32,2,8,256]{3,2,1,0:T(8,128)(2,1)}), bf16[32,2,8,256]{3,2,1,0:T(8,128)(2,1)S(1)}, u32[]{:S(2)}, u32[]{:S(2)}) async-start(bf16[32,2,8,256]{3,2,1,0:T(8,128)(2,1)} %prepare.1), calls=%async_computation | async-start | bytes 524288 | tf_op jit(solution)/shard_map/all_to_all | solution.py:322
  20.2 0.7 copy.19
  20.9 0.1 eq.34
  21.0 0.1 fusion.6
  21.1 1.3 %fusion.2 = f32[32]{0:T(128)S(1)} fusion(f32[32,8]{1,0:T(8,128)S(1)} %fusion.9.sign_ref, bf16[32,2048]{1,0:T(8,128)(2,1)} %bitcast.39, f32[1,2048,8]{1,2,0:T(8,128)} %param.10), kind=kOutput, calls=%fused_computation.5 | convolution fusion | flops 6291936 | bytes 197760 | tf_op jit(solution)/shard_map/dot_general | solution.py:336
  22.4 0.1 div.28
  22.5 0.1 squeeze.30
  22.6 0.1 squeeze.31
  22.7 0.1 fusion.10
  22.7 0.1 copy.23
  22.8 0.1 multiply_reduce_fusion
  22.9 0.0 copy-done
  23.0 1.2 fusion.3.step_ref
  24.2 3.7 %all-to-all-done.ur_ref = bf16[32,2,8,256]{3,2,1,0:T(8,128)(2,1)S(1)} async-done(((bf16[32,2,8,256]{3,2,1,0:T(8,128)(2,1)}), bf16[32,2,8,256]{3,2,1,0:T(8,128)(2,1)S(1)}, u32[]{:S(2)}, u32[]{:S(2)}) %all-to-all-start) | async-done | bytes 262176 | tf_op jit(solution)/shard_map/all_to_all | solution.py:322
  27.9 1.1 cascade.1._
  29.0 5.1 %all-to-all-start.1 = ((bf16[32,8,256]{2,1,0:T(8,128)(2,1)}), bf16[32,8,256]{2,1,0:T(8,128)(2,1)S(1)}, u32[]{:S(2)}, u32[]{:S(2)}) async-start(bf16[32,8,256]{2,1,0:T(8,128)(2,1)} %cascade.1._), calls=%async_computation.1 | async-start | bytes 262144 | tf_op jit(solution)/shard_map/all_to_all | solution.py:322
  34.1 0.0 copy-done.3
  34.1 0.0 copy-start.4
  34.1 0.9 copy-done.4
  35.0 0.5 fetch.1
  35.6 5.1 %all-to-all-done.1.cots_ref = bf16[32,8,256]{2,1,0:T(8,128)(2,1)S(1)} async-done(((bf16[32,8,256]{2,1,0:T(8,128)(2,1)}), bf16[32,8,256]{2,1,0:T(8,128)(2,1)S(1)}, u32[]{:S(2)}, u32[]{:S(2)}) %all-to-all-start.1) | async-done | bytes 131104 | tf_op jit(solution)/shard_map/all_to_all | solution.py:322
  40.7 0.8 middle.1
  41.5 79.9 %all-gather.2 = f16[768,2048]{1,0:T(8,128)(2,1)S(1)} all-gather(f16[24,2048]{1,0:T(8,128)(2,1)S(1)} %convert_element_type.34), channel_id=2, replica_groups=mesh['section'=32,'expert'=32] {'expert'}, dimensions={0}, use_global_device_ids=true | all-gather | bytes 3244032 | tf_op jit(solution)/shard_map/all_gather | solution.py:372
  121.5 0.1 slice.44
  121.6 0.4 fusion.1
  122.0 0.4 multiply_convert_fusion.slots_ref
  122.5 2.0 %finish.1 = (bf16[2,224,256]{2,1,0:T(8,128)(2,1)}, bf16[224,2048]{1,0:T(8,128)(2,1)}, f32[8,2048]{1,0:T(8,128)}, bf16[32,2048]{1,0:T(8,128)(2,1)}) custom-call(bf16[32,16,2048]{2,1,0:T(8,128)(2,1)S(1)} %multiply_convert_fusion.slots_ref, bf16[224,2048]{1,0:T(8,128)(2,1)S(1)} %get-tuple-element.13.weight_ref, ...), custom_call_target="tpu_custom_call" | custom-call | tf_op jit(solution)/shard_map/finish/pallas_call | solution.py:306
  (19 shorter events, 0.2 us)
Async XLA Ops:
  0.6 22.3 %copy-start = (bf16[2,16,2048]{2,1,0:T(8,128)(2,1)S(1)}, bf16[2,16,2048]{2,1,0:T(8,128)(2,1)}, u32[]{:S(2)}) copy-start(bf16[2,16,2048]{2,1,0:T(8,128)(2,1)} %param.7) | copy-start | bytes 393220
  0.6 40.0 %copy-start.1 = (bf16[1,2,16,2048]{3,2,1,0:T(8,128)(2,1)S(1)}, bf16[1,2,16,2048]{3,2,1,0:T(8,128)(2,1)}, u32[]{:S(2)}) copy-start(bf16[1,2,16,2048]{3,2,1,0:T(8,128)(2,1)} %param.8) | copy-start | bytes 393220
  0.7 40.0 %copy-start.2 = (bf16[1,2,16,2,2048]{4,3,2,1,0:T(2,128)(2,1)S(1)}, bf16[1,2,16,2,2048]{4,3,2,1,0:T(2,128)(2,1)}, u32[]{:S(2)}) copy-start(bf16[1,2,16,2,2048]{4,3,2,1,0:T(2,128)(2,1)} %param.9) | copy-start | bytes 786436
  0.7 33.4 %copy-start.3 = (bf16[1,224,2048]{2,1,0:T(8,128)(2,1)S(1)}, bf16[1,224,2048]{2,1,0:T(8,128)(2,1)}, u32[]{:S(2)}) copy-start(bf16[1,224,2048]{2,1,0:T(8,128)(2,1)} %param.13) | copy-start | bytes 2752516
  3.5 24.4 %all-to-all-start = ((bf16[32,2,8,256]{3,2,1,0:T(8,128)(2,1)}), bf16[32,2,8,256]{3,2,1,0:T(8,128)(2,1)S(1)}, u32[]{:S(2)}, u32[]{:S(2)}) async-start(bf16[32,2,8,256]{3,2,1,0:T(8,128)(2,1)} %prepare.1), calls=%async_computation | async-start | bytes 524288 | tf_op jit(solution)/shard_map/all_to_all | solution.py:322
  29.0 11.7 %all-to-all-start.1 = ((bf16[32,8,256]{2,1,0:T(8,128)(2,1)}), bf16[32,8,256]{2,1,0:T(8,128)(2,1)S(1)}, u32[]{:S(2)}, u32[]{:S(2)}) async-start(bf16[32,8,256]{2,1,0:T(8,128)(2,1)} %cascade.1._), calls=%async_computation.1 | async-start | bytes 262144 | tf_op jit(solution)/shard_map/all_to_all | solution.py:322
  34.1 0.9 copy-start.4
